TPU v7x, 32 devices: a whole 2x2x4 slice. The times are simulated.
32 devices in a mesh: fsdp: 4 (over y, x), rep: 8 (over z, core).
Axes of the slice: x: 2, y: 2, z: 4, core: 2. Of those that a mesh axis runs over, the one named last changes fastest.
Arguments:
- hidden_in: bfloat16 [8192, 2048], P(('fsdp', 'rep'))
- out_grad: bfloat16 [8192, 2048], P(('fsdp', 'rep')), may hold values from -6 to 6
- attn_saved: bfloat16 [8192, 256], P(('fsdp', 'rep')), may hold values from -6 to 6
- row_lse: float32 [8192, 2], P(('fsdp', 'rep')), may hold values from 2.5 to 6
- w_qkv: bfloat16 [2048, 512], P('fsdp'), may hold values from -0.125 to 0.125
- w_out_t: bfloat16 [2048, 256], P('fsdp'), may hold values from -0.125 to 0.125
- doc_lengths: int32 [32, 4], P(('fsdp', 'rep')), may hold values from 1 to 128, 256 in all within a row
- seq_start: int32 [32], P(('fsdp', 'rep')), may hold values from 0 to 2047
Outputs:
- input_grad: bfloat16 [8192, 2048], P(('fsdp', 'rep'))
- grad_update: float32 [2048, 768], P('fsdp')
- grad_norm: float32 [], replicated
Inputs may be any that keep to these rules, and one draw needn't show every extreme that they name: `doc_lengths`: each row sums to 256; the longest document of each device has exactly 128 tokens.
All inputs are finite; a program needn't handle non-finite values.
Results may differ from a plain program's by a relative error of at most 0.014.
Values may be sent and summed in bfloat16 or wider, within the bound.
No kernel may reach another device: no remote copies, remote signals or barrier semaphores. Data moves between devices by JAX's collectives and lax.ppermute only.
A program may use at most 64 MiB of HBM per device.

v0:
```python
import functools

import jax
import jax.numpy as jnp
from jax import lax
from jax.experimental import pallas as pl
from jax.experimental.pallas import tpu as pltpu
from jax.sharding import PartitionSpec as P


HEAD = 128


VMEM = pl.BlockSpec(memory_space=pltpu.VMEM)
SMEM = pl.BlockSpec(memory_space=pltpu.SMEM)


def dot(left, right):
    return jnp.dot(left, right, preferred_element_type=jnp.float32)


def contract_rows(left, right):
    return lax.dot_general(
        left, right, (((0,), (0,)), ((), ())), preferred_element_type=jnp.float32
    )


def contract_cols(left, right):
    return lax.dot_general(
        left, right, (((1,), (1,)), ((), ())), preferred_element_type=jnp.float32
    )


def shard_cols(index, mask, width):
    return pl.ds(pl.multiple_of(jnp.bitwise_xor(index, mask) * width, width), width)


def half_cols(core, width):
    return pl.ds(pl.multiple_of(core * width, width), width)


def halves_kernel(info, w_qkv, w_out, out):
    half, ohalf = w_qkv.shape[1] // 2, w_out.shape[1] // 2
    out[:, :half] = w_qkv[:, half_cols(info[1], half)]
    out[:, half:] = w_out[:, half_cols(info[1], ohalf)]


def out_terms_kernel(shards, info, out_grad, saved, keep, send):
    width = out_grad.shape[1] // shards
    half = saved.shape[1] // 2
    index, core = info[0], info[1]
    own = saved[:, half_cols(core, half)]
    other = saved[:, half_cols(1 - core, half)]
    for mask in range(shards):
        part = out_grad[:, shard_cols(index, mask, width)]
        keep[mask] = contract_rows(part, own).astype(jnp.bfloat16)
        send[mask] = contract_rows(part, other).astype(jnp.bfloat16)


def attention_kernel(shards, info, hidden, out_grad, saved, lse, cosine, sines, allowed, w_qkv,
                     w_out, *rest):
    mine = rest[: shards - 1]
    theirs = rest[shards - 1 : 2 * shards - 2]
    d_qkv = rest[2 * shards - 2]
    outs = rest[2 * shards - 1 : -2]
    proj, attn = rest[-2:]
    index, core = info[0], info[1]
    width = hidden.shape[1] // shards
    half = w_qkv.shape[1] // 2
    ohalf = w_out.shape[1] // 2
    heads = lse.shape[1]
    scale = 1.0 / HEAD**0.5
    own_cols = shard_cols(index, 0, width)
    proj[...] = dot(hidden[:, own_cols], w_qkv[...])
    attn[...] = dot(out_grad[:, own_cols], w_out[...])
    for chunks, side in ((mine, core), (theirs, 1 - core)):
        cols, ocols = half_cols(side, half), half_cols(side, ohalf)
        acc, oacc = proj[:, cols], attn[:, ocols]
        for mask in range(1, shards):
            sel = shard_cols(index, mask, width)
            chunk = chunks[mask - 1]
            acc += dot(hidden[:, sel], chunk[:, :half])
            oacc += dot(out_grad[:, sel], chunk[:, half:])
        proj[:, cols] = acc
        attn[:, ocols] = oacc
    cos, sin = cosine[...], sines[...]

    def turn(block, sign):
        return block * cos + sign * pltpu.roll(block, HEAD // 2, 1) * sin

    query_width = heads * HEAD
    keys = turn(proj[:, query_width : query_width + HEAD], 1.0).astype(jnp.bfloat16)
    values = proj[:, query_width + HEAD :].astype(jnp.bfloat16)
    see = allowed[...] > 0.0
    key_grad = jnp.zeros((hidden.shape[0], HEAD), jnp.float32)
    value_grad = jnp.zeros((hidden.shape[0], HEAD), jnp.float32)
    for head in range(heads):
        span = slice(head * HEAD, (head + 1) * HEAD)
        query = turn(proj[:, span], 1.0).astype(jnp.bfloat16)
        grad = attn[:, span].astype(jnp.bfloat16)
        scores = contract_cols(query, keys) * scale
        probs = jnp.where(see, jnp.exp(scores - lse[:, head : head + 1]), 0.0)
        dprobs = contract_cols(grad, values)
        delta = jnp.sum(
            grad.astype(jnp.float32) * saved[:, span].astype(jnp.float32), axis=1, keepdims=True
        )
        dscores = (probs * (dprobs - delta) * scale).astype(jnp.bfloat16)
        value_grad += contract_rows(probs.astype(jnp.bfloat16), grad)
        key_grad += contract_rows(dscores, query)
        d_qkv[:, span] = turn(dot(dscores, keys), -1.0).astype(jnp.bfloat16)
    d_qkv[:, query_width : query_width + HEAD] = turn(key_grad, -1.0).astype(jnp.bfloat16)
    d_qkv[:, query_width + HEAD :] = value_grad.astype(jnp.bfloat16)
    own = d_qkv[:, half_cols(core, half)]
    other = d_qkv[:, half_cols(1 - core, half)]
    for mask in range(shards):
        part = hidden[:, shard_cols(index, mask, width)]
        outs[mask][...] = contract_rows(part, own).astype(jnp.bfloat16)
        outs[shards + mask][...] = contract_rows(part, other).astype(jnp.bfloat16)


def input_kernel(shards, info, d_qkv, w_qkv, *rest):
    mine = rest[: shards - 1]
    theirs = rest[shards - 1 : 2 * shards - 2]
    out = rest[-1]
    index, core = info[0], info[1]
    width = w_qkv.shape[0]
    half = w_qkv.shape[1] // 2
    out[:, shard_cols(index, 0, width)] = contract_cols(d_qkv[...], w_qkv[...]).astype(out.dtype)
    own = d_qkv[:, half_cols(core, half)]
    other = d_qkv[:, half_cols(1 - core, half)]
    for mask in range(1, shards):
        total = contract_cols(own, mine[mask - 1][:, :half])
        total += contract_cols(other, theirs[mask - 1][:, :half])
        out[:, shard_cols(index, mask, width)] = total.astype(out.dtype)


def gather_kernel(info, *rest):
    pieces, own, square = rest[:-2], rest[-2], rest[-1]
    rows = pieces[0].shape[0]
    for mask, piece in enumerate(pieces):
        spot = jnp.bitwise_xor(info[2], mask) * rows
        own[pl.ds(pl.multiple_of(spot, rows), rows), :] = piece[...]
    total = jnp.sum(jnp.square(own[...].astype(jnp.float32)))
    square[...] = jnp.full(square.shape, total, jnp.float32)


def finish_kernel(count, half, info, own, other, line, away, out, norm):
    norm_sq = line[...] + away[...]
    scale = lax.rsqrt(norm_sq / count + 1e-06)
    norm[...] = jnp.sqrt(norm_sq)
    ohalf = own.shape[1] - half
    core, lanes = info[1], scale.shape[1]
    for part, side in ((own, core), (other, 1 - core)):
        for lower in range(0, half, lanes):
            spot = pl.ds(pl.multiple_of(side * half + lower, lanes), lanes)
            out[:, spot] = part[:, lower : lower + lanes].astype(jnp.float32) * scale
        for lower in range(0, ohalf, lanes):
            spot = pl.ds(pl.multiple_of(2 * half + side * ohalf + lower, lanes), lanes)
            block = part[:, half + lower : half + lower + lanes]
            out[:, spot] = block.astype(jnp.float32) * scale


def vmem_call(kernel, outs, scratch=()):
    def run(info, *args):
        return call(info, *args)

    def call(info, *args):
        return pl.pallas_call(
            kernel,
            out_shape=outs,
            in_specs=[SMEM] + [VMEM] * len(args),
            out_specs=jax.tree.map(lambda _: VMEM, outs),
            scratch_shapes=list(scratch),
        )(info, *args)

    return run


def arrange(pieces, place):
    stacked = jnp.stack(pieces)
    count = len(pieces)
    bit = 1
    while bit < count:
        shape = stacked.shape
        split = stacked.reshape((count // (2 * bit), 2, bit) + shape[1:])
        swapped = jnp.concatenate([split[:, 1:], split[:, :1]], axis=1)
        stacked = jnp.where((place & bit) != 0, swapped, split).reshape(shape)
        bit *= 2
    return stacked.reshape((count * pieces[0].shape[0],) + pieces[0].shape[1:])


def tree_sum(parts):
    while len(parts) > 1:
        parts = [left + right for left, right in zip(parts[::2], parts[1::2])]
    return parts[0]


def body(shards, copies, hidden_in, out_grad, attn_saved, row_lse, w_qkv, w_out_t, doc_lengths,
         seq_start):
    rows = hidden_in.shape[0]
    bf16 = jnp.bfloat16
    groups = copies // 2
    index = lax.axis_index("fsdp")
    member = lax.axis_index("rep")
    core = member % 2
    place = member // 2
    info = jnp.stack([index, core, place]).astype(jnp.int32)
    half, ohalf = w_qkv.shape[1] // 2, w_out_t.shape[1] // 2
    width = w_qkv.shape[0]

    def to_shard(value, mask):
        return lax.ppermute(value, "fsdp", [(i, i ^ mask) for i in range(shards)])

    def to_member(value, mask):
        return lax.ppermute(value, "rep", [(i, i ^ mask) for i in range(copies)])

    first = vmem_call(
        halves_kernel, jax.ShapeDtypeStruct((width, half + ohalf), bf16)
    )(info, w_qkv, w_out_t)
    mine = [to_shard(first, mask) for mask in range(1, shards)]

    positions = seq_start[0] + jnp.arange(rows, dtype=jnp.int32)
    half_size = HEAD // 2
    inverse = 1000000.0 ** (-(jnp.arange(half_size, dtype=jnp.float32) * 2.0) / HEAD)
    angles = positions.astype(jnp.float32)[:, None] * inverse[None, :]
    cosine, sines = jnp.cos(angles), jnp.sin(angles)
    cosine = jnp.concatenate([cosine, cosine], axis=1)
    sines = jnp.concatenate([-sines, sines], axis=1)
    local = jnp.arange(rows, dtype=jnp.int32)
    ends = jnp.cumsum(doc_lengths[0])
    documents = jnp.sum((local[:, None] >= ends[None, :]).astype(jnp.int32), axis=1)
    allowed = (
        (documents[:, None] == documents[None, :]) & (local[None, :] <= local[:, None])
    ).astype(jnp.float32)

    out_shape = jax.ShapeDtypeStruct((shards, width, ohalf), bf16)
    out_keep, out_send = vmem_call(
        functools.partial(out_terms_kernel, shards), [out_shape] * 2
    )(info, out_grad, attn_saved)
    out_sum = out_keep.astype(jnp.float32) + to_member(out_send, 1).astype(jnp.float32)
    out_low = [out_sum[mask].astype(bf16) for mask in range(1, shards)]
    out_low, fence = lax.optimization_barrier((out_low, mine))
    theirs = [to_member(chunk, 1) for chunk in fence]
    out_got = [to_shard(low, mask + 1) for mask, low in enumerate(out_low)]

    qkv_shape = jax.ShapeDtypeStruct((width, half), bf16)
    results = vmem_call(
        functools.partial(attention_kernel, shards),
        [jax.ShapeDtypeStruct((rows, w_qkv.shape[1]), bf16)] + [qkv_shape] * (2 * shards),
        [
            pltpu.VMEM((rows, w_qkv.shape[1]), jnp.float32),
            pltpu.VMEM((rows, w_out_t.shape[1]), jnp.float32),
        ],
    )(info, hidden_in, out_grad, attn_saved, row_lse, cosine, sines, allowed, w_qkv, w_out_t,
      *fence, *theirs)
    d_qkv, keep, send = results[0], results[1 : shards + 1], results[shards + 1 :]
    input_grad = vmem_call(
        functools.partial(input_kernel, shards), jax.ShapeDtypeStruct(hidden_in.shape, bf16)
    )(info, d_qkv, w_qkv, *fence, *theirs)

    qkv_got = []
    for mask in list(range(1, shards)) + [0]:
        both = keep[mask].astype(jnp.float32) + to_member(send[mask], 1).astype(jnp.float32)
        qkv_got.append(to_shard(both.astype(bf16), mask) if mask else both)
    qkv_got, out_got, input_grad = lax.optimization_barrier((qkv_got, out_got, input_grad))
    total = jnp.concatenate(
        [
            sum(part.astype(jnp.float32) for part in qkv_got),
            sum((part.astype(jnp.float32) for part in out_got), out_sum[0]),
        ],
        axis=1,
    )
    low = total.astype(bf16)
    piece_rows = width // groups
    piece = lax.dynamic_slice_in_dim(total, place * piece_rows, piece_rows, 0)
    for mask in range(1, groups):
        away = lax.dynamic_slice_in_dim(low, (place ^ mask) * piece_rows, piece_rows, 0)
        piece = piece + to_member(away, 2 * mask).astype(jnp.float32)
    low = piece.astype(bf16)
    pieces = [low] + [to_member(low, 2 * mask) for mask in range(1, groups)]
    columns = half + ohalf
    line_shape = jax.ShapeDtypeStruct((1, 128), jnp.float32)
    if piece_rows % 16 == 0:
        own, square = vmem_call(
            gather_kernel, [jax.ShapeDtypeStruct((width, columns), bf16), line_shape]
        )(info, *pieces)
    else:
        own = arrange(pieces, place)
        square = jnp.sum(jnp.square(own.astype(jnp.float32)))
        square = jnp.full((1, 128), square, jnp.float32)
    other = to_member(own, 1)
    line = tree_sum([square] + [to_shard(square, mask) for mask in range(1, shards)])
    away = to_member(line, 1)
    grad_update, norm = vmem_call(
        functools.partial(finish_kernel, float(width * shards * 2 * columns), half),
        [jax.ShapeDtypeStruct((width, 2 * columns), jnp.float32), line_shape],
    )(info, own, other, line, away)
    return (input_grad, grad_update, norm[0, 0])


def solution(mesh):
    in_specs = (
        P(("fsdp", "rep"), None),
        P(("fsdp", "rep"), None),
        P(("fsdp", "rep"), None),
        P(("fsdp", "rep"), None),
        P("fsdp", None),
        P("fsdp", None),
        P(("fsdp", "rep"), None),
        P(("fsdp", "rep")),
    )
    out_specs = (P(("fsdp", "rep"), None), P("fsdp", None), P())

    def run(*args):
        return body(mesh.shape["fsdp"], mesh.shape["rep"], *args)

    return jax.shard_map(run, mesh=mesh, in_specs=in_specs, out_specs=out_specs, check_vma=False)
```

profile of v0, /device:TPU:0, one launch (start us, length us, event | category | flops | bytes accessed | tf_op | source)
XLA Modules:
  0.0 102.6 jit_solution(18156213005084034330)
XLA Ops:
  0.7 0.7 pad_add_fusion.info
  1.3 3.0 %shard_map.103 = (bf16[4,512,128]{2,1,0:T(8,128)(2,1)}, bf16[4,512,128]{2,1,0:T(8,128)(2,1)}) custom-call(s32[3]{0:T(128)} %pad_add_fusion.info, bf16[256,2048]{1,0:T(8,128)(2,1)} %out_grad.3, bf16[256,256]{1,0:T(8,128)(2,1)} %saved.3), custom_call_target="tpu_custom_call" | custom-call | tf_op jit(solution)/shard_map/pallas_call | solution.py:168
  4.8 1.9 %shard_map.104 = bf16[512,384]{1,0:T(8,128)(2,1)} custom-call(s32[3]{0:T(128)} %pad_add_fusion.info, bf16[512,512]{1,0:T(8,128)(2,1)} %w_qkv.5, bf16[512,256]{1,0:T(8,128)(2,1)} %w_out.3), custom_call_target="tpu_custom_call" | custom-call | tf_op jit(solution)/shard_map/pallas_call | solution.py:168
  6.7 2.5 %collective-permute-start.1 = (bf16[512,384]{1,0:T(8,128)(2,1)}, bf16[512,384]{1,0:T(8,128)(2,1)S(1)}, u32[]{:S(2)}, u32[]{:S(2)}) collective-permute-start(bf16[512,384]{1,0:T(8,128)(2,1)} %shard_map.104), channel_id=1, source_target_pairs={{0,8},{8,0},{16,24},{24,16},{1,9},{9,1},{17,25},{25,17},{2,10},{10... | collective-permute-start | bytes 1179656 | tf_op jit(solution)/shard_map/ppermute | solution.py:212
  9.3 1.5 %collective-permute-start.2 = (bf16[512,384]{1,0:T(8,128)(2,1)}, bf16[512,384]{1,0:T(8,128)(2,1)S(1)}, u32[]{:S(2)}, u32[]{:S(2)}) collective-permute-start(bf16[512,384]{1,0:T(8,128)(2,1)} %shard_map.104), channel_id=1, source_target_pairs={{0,16},{8,24},{16,0},{24,8},{1,17},{9,25},{17,1},{25,9},{2,18},{10... | collective-permute-start | bytes 1179656 | tf_op jit(solution)/shard_map/ppermute | solution.py:212
  11.6 1.3 %fusion.11 = (f32[256,64]{1,0:T(8,128)S(1)}, f32[256,64]{1,0:T(8,128)}, f32[256,64]{1,0:T(8,128)}) fusion(f32[64]{0:T(128)S(1)} %multiply_power_fusion, f32[256]{0:T(256)S(1)} %add_convert_fusion.3), kind=kLoop, calls=%fused_computation.29 | loop fusion | flops 32768 | bytes 197888 | tf_op jit(solution)/shard_map/neg | solution.py:228
  13.0 0.8 slice_bitcast_fusion.1
  13.8 5.6 %collective-permute-done.1.rest_0_ = bf16[512,384]{1,0:T(8,128)(2,1)S(1)} collective-permute-done((bf16[512,384]{1,0:T(8,128)(2,1)}, bf16[512,384]{1,0:T(8,128)(2,1)S(1)}, u32[]{:S(2)}, u32[]{:S(2)}) %collective-permute-start.1) | collective-permute-done | bytes 393248 | tf_op jit(solution)/shard_map/ppermute | solution.py:212
  19.4 9.7 %collective-permute-done.2.rest_1_ = bf16[512,384]{1,0:T(8,128)(2,1)S(1)} collective-permute-done((bf16[512,384]{1,0:T(8,128)(2,1)}, bf16[512,384]{1,0:T(8,128)(2,1)S(1)}, u32[]{:S(2)}, u32[]{:S(2)}) %collective-permute-start.2) | collective-permute-done | bytes 393248 | tf_op jit(solution)/shard_map/ppermute | solution.py:212
  29.2 0.5 collective-permute-start.5
  29.8 0.8 copy.12.lse
  30.6 1.9 %pad_maximum_fusion.1 = (f32[256,128]{1,0:T(8,128)}, f32[256,128]{1,0:T(8,128)}) fusion(f32[256,64]{1,0:T(8,128)} %get-tuple-element.71, f32[256,64]{1,0:T(8,128)} %get-tuple-element.70, f32[256,64]{1,0:T(8,128)S(1)} %get-tuple-element.69), kind=kLoop, calls=%fused_computation.27 | loop fusion | flops 65536 | bytes 458752 | tf_op jit(solution)/shard_map/concatenate | solution.py:227
  32.5 0.8 fusion.5.allowed
  33.4 0.7 copy-done.3
  34.3 6.5 %shard_map.105 = (bf16[256,512]{1,0:T(8,128)(2,1)}, bf16[512,256]{1,0:T(8,128)(2,1)}, bf16[512,256]{1,0:T(8,128)(2,1)}, bf16[512,256]{1,0:T(8,128)(2,1)}, bf16[5...) custom-call(s32[3]{0:T(128)} %pad_add_fusion.info, ...), custom_call_target="tpu_custom_call" | custom-call | tf_op jit(solution)/shard_map/pallas_call | solution.py:168
  40.9 0.5 collective-permute-start.7
  41.4 1.2 %collective-permute-start.14 = (bf16[512,128]{1,0:T(8,128)(2,1)}, bf16[512,128]{1,0:T(8,128)(2,1)S(1)}, u32[]{:S(2)}, u32[]{:S(2)}) collective-permute-start(bf16[512,128]{1,0:T(8,128)(2,1)} %get-tuple-element.45), channel_id=1, source_target_pairs={{0,8},{8,0},{16,24},{24,16},{1,9},{9,1},{17,25},{25,17},{2,10},{10... | collective-permute-start | bytes 393224 | tf_op jit(solution)/shard_map/ppermute | solution.py:212
  43.1 1.0 add_convert_fusion.2
  44.1 0.9 collective-permute-start.8
  45.1 1.0 add_convert_fusion.1
  46.1 1.6 %collective-permute-start.10 = (bf16[512,256]{1,0:T(8,128)(2,1)S(1)}, bf16[512,256]{1,0:T(8,128)(2,1)S(1)}, u32[]{:S(2)}, u32[]{:S(2)}) collective-permute-start(bf16[512,256]{1,0:T(8,128)(2,1)S(1)} %add_convert_fusion.1), channel_id=1, source_target_pairs={{0,16},{8,24},{16,0},{24,8},{1,17},{9,25},{17,1},{25,9},{2,18},{10... | collective-permute-start | bytes 786440 | tf_op jit(solution)/shard_map/ppermute | solution.py:212
  47.7 1.2 %collective-permute-start.12 = (bf16[512,256]{1,0:T(8,128)(2,1)S(1)}, bf16[512,256]{1,0:T(8,128)(2,1)S(1)}, u32[]{:S(2)}, u32[]{:S(2)}) collective-permute-start(bf16[512,256]{1,0:T(8,128)(2,1)S(1)} %add_convert_fusion), channel_id=1, source_target_pairs={{0,24},{8,16},{16,8},{24,0},{1,25},{9,17},{17,9},{25,1},{2,26},{10... | collective-permute-start | bytes 786440 | tf_op jit(solution)/shard_map/ppermute | solution.py:212
  48.9 3.6 %shard_map.106 = bf16[256,2048]{1,0:T(8,128)(2,1)} custom-call(s32[3]{0:T(128)} %pad_add_fusion.info, bf16[256,512]{1,0:T(8,128)(2,1)} %get-tuple-element.48.d_qkv, bf16[512,512]{1,0:T(8,128)(2,1)} %w_qkv.5, bf16[512,384]{1,0:T(8,128)(2,1)} %copy-done, bf16[512,384]{1,0:T(8,128)(2,1)} %copy-done.1, bf16[512,384]{1,0:T(8,128)(2,1)} %copy-done.2, ...), custom_call_target="tpu_custom_call" | custom-call | tf_op jit(solution)/shard_map/pallas_call | solution.py:168
  52.5 1.2 %collective-permute-start.15 = (bf16[512,128]{1,0:T(8,128)(2,1)S(1)}, bf16[512,128]{1,0:T(8,128)(2,1)S(1)}, u32[]{:S(2)}, u32[]{:S(2)}) collective-permute-start(bf16[512,128]{1,0:T(8,128)(2,1)S(1)} %copy-done.12), channel_id=1, source_target_pairs={{0,16},{8,24},{16,0},{24,8},{1,17},{9,25},{17,1},{25,9},{2,18},{10... | collective-permute-start | bytes 393224 | tf_op jit(solution)/shard_map/ppermute | solution.py:212
  53.8 1.2 %collective-permute-start.16 = (bf16[512,128]{1,0:T(8,128)(2,1)S(1)}, bf16[512,128]{1,0:T(8,128)(2,1)S(1)}, u32[]{:S(2)}, u32[]{:S(2)}) collective-permute-start(bf16[512,128]{1,0:T(8,128)(2,1)S(1)} %copy-done.11), channel_id=1, source_target_pairs={{0,24},{8,16},{16,8},{24,0},{1,25},{9,17},{17,9},{25,1},{2,26},{10... | collective-permute-start | bytes 393224 | tf_op jit(solution)/shard_map/ppermute | solution.py:212
  55.0 10.6 %collective-permute-done.15 = bf16[512,128]{1,0:T(8,128)(2,1)S(1)} collective-permute-done((bf16[512,128]{1,0:T(8,128)(2,1)S(1)}, bf16[512,128]{1,0:T(8,128)(2,1)S(1)}, u32[]{:S(2)}, u32[]{:S(2)}) %collective-permute-start.15) | collective-permute-done | bytes 131104 | tf_op jit(solution)/shard_map/ppermute | solution.py:212
  65.9 3.7 %collective-permute-start.19 = (bf16[128,384]{1,0:T(8,128)(2,1)S(1)}, bf16[128,384]{1,0:T(8,128)(2,1)S(1)}, u32[]{:S(2)}, u32[]{:S(2)}) collective-permute-start(bf16[128,384]{1,0:T(8,128)(2,1)S(1)} %get-tuple-element.67), channel_id=1, source_target_pairs={{0,6},{1,7},{2,4},{3,5},{4,2},{5,3},{6,0},{7,1},{8,14},{9,15},{10,... | collective-permute-start | bytes 294920 | tf_op jit(solution)/shard_map/ppermute | solution.py:215
  69.6 0.8 collective-permute-start.17
  70.4 2.9 %collective-permute-done.19 = bf16[128,384]{1,0:T(8,128)(2,1)S(1)} collective-permute-done((bf16[128,384]{1,0:T(8,128)(2,1)S(1)}, bf16[128,384]{1,0:T(8,128)(2,1)S(1)}, u32[]{:S(2)}, u32[]{:S(2)}) %collective-permute-start.19) | collective-permute-done | bytes 98336 | tf_op jit(solution)/shard_map/ppermute | solution.py:215
  73.3 4.5 %collective-permute-done.18 = bf16[128,384]{1,0:T(8,128)(2,1)S(1)} collective-permute-done((bf16[128,384]{1,0:T(8,128)(2,1)S(1)}, bf16[128,384]{1,0:T(8,128)(2,1)S(1)}, u32[]{:S(2)}, u32[]{:S(2)}) %collective-permute-start.18) | collective-permute-done | bytes 98336 | tf_op jit(solution)/shard_map/ppermute | solution.py:215
  77.8 0.6 collective-permute-start.20
  78.4 2.6 %collective-permute-start.21 = (bf16[128,384]{1,0:T(8,128)(2,1)S(1)}, bf16[128,384]{1,0:T(8,128)(2,1)S(1)}, u32[]{:S(2)}, u32[]{:S(2)}) collective-permute-start(bf16[128,384]{1,0:T(8,128)(2,1)S(1)} %fusion.10.rest_0_), channel_id=1, source_target_pairs={{0,4},{1,5},{2,6},{3,7},{4,0},{5,1},{6,2},{7,3},{8,12},{9,13},{10,... | collective-permute-start | bytes 294920 | tf_op jit(solution)/shard_map/ppermute | solution.py:215
  81.0 1.3 %collective-permute-start.22 = (bf16[128,384]{1,0:T(8,128)(2,1)S(1)}, bf16[128,384]{1,0:T(8,128)(2,1)S(1)}, u32[]{:S(2)}, u32[]{:S(2)}) collective-permute-start(bf16[128,384]{1,0:T(8,128)(2,1)S(1)} %fusion.10.rest_0_), channel_id=1, source_target_pairs={{0,6},{1,7},{2,4},{3,5},{4,2},{5,3},{6,0},{7,1},{8,14},{9,15},{10,... | collective-permute-start | bytes 294920 | tf_op jit(solution)/shard_map/ppermute | solution.py:215
  82.3 0.5 collective-permute-done.20.rest_1_
  82.8 5.2 %collective-permute-done.21.rest_2_ = bf16[128,384]{1,0:T(8,128)(2,1)S(1)} collective-permute-done((bf16[128,384]{1,0:T(8,128)(2,1)S(1)}, bf16[128,384]{1,0:T(8,128)(2,1)S(1)}, u32[]{:S(2)}, u32[]{:S(2)}) %collective-permute-start.21) | collective-permute-done | bytes 98336 | tf_op jit(solution)/shard_map/ppermute | solution.py:215
  88.0 0.6 copy-done.14
  88.7 0.6 copy-done.15
  89.3 1.9 %shard_map.107 = (bf16[512,384]{1,0:T(8,128)(2,1)}, f32[1,128]{1,0:T(1,128)}) custom-call(s32[3]{0:T(128)} %pad_add_fusion.info, bf16[128,384]{1,0:T(8,128)(2,1)} %copy-done.7, bf16[128,384]{1,0:T(8,128)(2,1)} %copy-done.13, bf16[128,384]{1,0:T(8,128)(2,1)} %copy-done.14, bf16[128,384]{1,0:T(8,128)(2,1)} %copy-done.15), custom_call_target="tpu_custom_call" | custom-call | tf_op jit(solution)/shard_map/pallas_call | solution.py:168
  91.2 0.7 collective-permute-start.25
  91.9 1.5 %collective-permute-start.26 = (f32[1,128]{1,0:T(1,128)}, f32[1,128]{1,0:T(1,128)S(1)}, u32[]{:S(2)}, u32[]{:S(2)}) collective-permute-start(f32[1,128]{1,0:T(1,128)} %get-tuple-element.58), channel_id=1, source_target_pairs={{0,24},{8,16},{16,8},{24,0},{1,25},{9,17},{17,9},{25,1},{2,26},{10... | collective-permute-start | bytes 1544 | tf_op jit(solution)/shard_map/ppermute | solution.py:212
  93.3 1.4 %collective-permute-start.24 = (f32[1,128]{1,0:T(1,128)}, f32[1,128]{1,0:T(1,128)S(1)}, u32[]{:S(2)}, u32[]{:S(2)}) collective-permute-start(f32[1,128]{1,0:T(1,128)} %get-tuple-element.58), channel_id=1, source_target_pairs={{0,8},{8,0},{16,24},{24,16},{1,9},{9,1},{17,25},{25,17},{2,10},{10... | collective-permute-start | bytes 1544 | tf_op jit(solution)/shard_map/ppermute | solution.py:212
  94.9 1.6 %collective-permute-done.26 = f32[1,128]{1,0:T(1,128)S(1)} collective-permute-done((f32[1,128]{1,0:T(1,128)}, f32[1,128]{1,0:T(1,128)S(1)}, u32[]{:S(2)}, u32[]{:S(2)}) %collective-permute-start.26) | collective-permute-done | bytes 544 | tf_op jit(solution)/shard_map/ppermute | solution.py:212
  96.5 0.6 collective-permute-done.24
  97.0 0.7 add_add_fusion.1.line
  97.7 1.2 %collective-permute-done.27.away = f32[1,128]{1,0:T(1,128)S(1)} collective-permute-done((f32[1,128]{1,0:T(1,128)S(1)}, f32[1,128]{1,0:T(1,128)S(1)}, u32[]{:S(2)}, u32[]{:S(2)}) %collective-permute-start.27) | collective-permute-done | bytes 544 | tf_op jit(solution)/shard_map/ppermute | solution.py:215
  98.9 0.6 copy-done.18
  99.5 0.8 copy-done.8
  100.2 2.4 %shard_map.108 = (f32[512,768]{1,0:T(8,128)}, f32[1,128]{1,0:T(1,128)}) custom-call(s32[3]{0:T(128)} %pad_add_fusion.info, bf16[512,384]{1,0:T(8,128)(2,1)} %get-tuple-element.57.own, bf16[512,384]{1,0:T(8,128)(2,1)} %copy-done.8, f32[1,128]{1,0:T(1,128)} %copy-done.17, f32[1,128]{1,0:T(1,128)} %copy-done.18), custom_call_target="tpu_custom_call" | custom-call | tf_op jit(solution)/shard_map/pallas_call | solution.py:168
  (75 shorter events, 2.7 us)
Async XLA Ops:
  0.6 10.8 %copy-start.19 = (s32[1,4]{1,0:T(1,128)S(1)}, s32[1,4]{1,0:T(1,128)}, u32[]{:S(2)}) copy-start(s32[1,4]{1,0:T(1,128)} %param.14) | copy-start | bytes 52
  4.3 8.6 %copy-start.6 = (bf16[4,512,128]{2,1,0:T(8,128)(2,1)S(1)}, bf16[4,512,128]{2,1,0:T(8,128)(2,1)}, u32[]{:S(2)}) copy-start(bf16[4,512,128]{2,1,0:T(8,128)(2,1)} %get-tuple-element.32) | copy-start | bytes 1572868
  4.3 8.6 %collective-permute-start = (bf16[4,512,128]{2,1,0:T(8,128)(2,1)}, bf16[4,512,128]{2,1,0:T(8,128)(2,1)S(1)}, u32[]{:S(2)}, u32[]{:S(2)}) collective-permute-start(bf16[4,512,128]{2,1,0:T(8,128)(2,1)} %get-tuple-element.33), channel_id=1, source_target_pairs={{0,1},{1,0},{2,3},{3,2},{4,5},{5,4},{6,7},{7,6},{8,9},{9,8},{10,11... | collective-permute-start | bytes 1572872 | tf_op jit(solution)/shard_map/ppermute | solution.py:215
  6.7 12.7 %collective-permute-start.1 = (bf16[512,384]{1,0:T(8,128)(2,1)}, bf16[512,384]{1,0:T(8,128)(2,1)S(1)}, u32[]{:S(2)}, u32[]{:S(2)}) collective-permute-start(bf16[512,384]{1,0:T(8,128)(2,1)} %shard_map.104), channel_id=1, source_target_pairs={{0,8},{8,0},{16,24},{24,16},{1,9},{9,1},{17,25},{25,17},{2,10},{10... | collective-permute-start | bytes 1179656 | tf_op jit(solution)/shard_map/ppermute | solution.py:212
  9.3 19.8 %collective-permute-start.2 = (bf16[512,384]{1,0:T(8,128)(2,1)}, bf16[512,384]{1,0:T(8,128)(2,1)S(1)}, u32[]{:S(2)}, u32[]{:S(2)}) collective-permute-start(bf16[512,384]{1,0:T(8,128)(2,1)} %shard_map.104), channel_id=1, source_target_pairs={{0,16},{8,24},{16,0},{24,8},{1,17},{9,25},{17,1},{25,9},{2,18},{10... | collective-permute-start | bytes 1179656 | tf_op jit(solution)/shard_map/ppermute | solution.py:212
  10.8 18.3 %collective-permute-start.3 = (bf16[512,384]{1,0:T(8,128)(2,1)}, bf16[512,384]{1,0:T(8,128)(2,1)S(1)}, u32[]{:S(2)}, u32[]{:S(2)}) collective-permute-start(bf16[512,384]{1,0:T(8,128)(2,1)} %shard_map.104), channel_id=1, source_target_pairs={{0,24},{8,16},{16,8},{24,0},{1,25},{9,17},{17,9},{25,1},{2,26},{10... | collective-permute-start | bytes 1179656 | tf_op jit(solution)/shard_map/ppermute | solution.py:212
  12.9 16.9 %copy-start.16 = (f32[256,2]{0,1:T(2,128)S(1)}, f32[256,2]{0,1:T(2,128)}, u32[]{:S(2)}) copy-start(f32[256,2]{0,1:T(2,128)} %param.11) | copy-start | bytes 6148
  19.4 13.9 %copy-start = (bf16[512,384]{1,0:T(8,128)(2,1)}, bf16[512,384]{1,0:T(8,128)(2,1)S(1)}, u32[]{:S(2)}) copy-start(bf16[512,384]{1,0:T(8,128)(2,1)S(1)} %collective-permute-done.1.rest_0_) | copy-start | bytes 1179652
  29.1 4.3 %copy-start.1 = (bf16[512,384]{1,0:T(8,128)(2,1)}, bf16[512,384]{1,0:T(8,128)(2,1)S(1)}, u32[]{:S(2)}) copy-start(bf16[512,384]{1,0:T(8,128)(2,1)S(1)} %collective-permute-done.2.rest_1_) | copy-start | bytes 1179652
  29.1 4.3 %copy-start.2 = (bf16[512,384]{1,0:T(8,128)(2,1)}, bf16[512,384]{1,0:T(8,128)(2,1)S(1)}, u32[]{:S(2)}) copy-start(bf16[512,384]{1,0:T(8,128)(2,1)S(1)} %collective-permute-done.3.rest_2_) | copy-start | bytes 1179652
  29.1 4.2 %collective-permute-start.4 = (bf16[512,384]{1,0:T(8,128)(2,1)S(1)}, bf16[512,384]{1,0:T(8,128)(2,1)S(1)}, u32[]{:S(2)}, u32[]{:S(2)}) collective-permute-start(bf16[512,384]{1,0:T(8,128)(2,1)S(1)} %collective-permute-done.1.rest_0_), channel_id=1, source_target_pairs={{0,1},{1,0},{2,3},{3,2},{4,5},{5,4},{6,7},{7,6},{8,9},{9,8},{10,11... | collective-permute-start | bytes 1179656 | tf_op jit(solution)/shard_map/ppermute | solution.py:215
  29.2 4.2 %collective-permute-start.5 = (bf16[512,384]{1,0:T(8,128)(2,1)S(1)}, bf16[512,384]{1,0:T(8,128)(2,1)S(1)}, u32[]{:S(2)}, u32[]{:S(2)}) collective-permute-start(bf16[512,384]{1,0:T(8,128)(2,1)S(1)} %collective-permute-done.2.rest_1_), channel_id=1, source_target_pairs={{0,1},{1,0},{2,3},{3,2},{4,5},{5,4},{6,7},{7,6},{8,9},{9,8},{10,11... | collective-permute-start | bytes 1179656 | tf_op jit(solution)/shard_map/ppermute | solution.py:215
  29.7 3.7 %collective-permute-start.6 = (bf16[512,384]{1,0:T(8,128)(2,1)S(1)}, bf16[512,384]{1,0:T(8,128)(2,1)S(1)}, u32[]{:S(2)}, u32[]{:S(2)}) collective-permute-start(bf16[512,384]{1,0:T(8,128)(2,1)S(1)} %collective-permute-done.3.rest_2_), channel_id=1, source_target_pairs={{0,1},{1,0},{2,3},{3,2},{4,5},{5,4},{6,7},{7,6},{8,9},{9,8},{10,11... | collective-permute-start | bytes 1179656 | tf_op jit(solution)/shard_map/ppermute | solution.py:215
  33.3 0.8 copy-start.3
  33.3 0.9 copy-start.4
  33.3 1.0 copy-start.5
  40.9 6.8 %copy-start.9 = (bf16[512,256]{1,0:T(8,128)(2,1)S(1)}, bf16[512,256]{1,0:T(8,128)(2,1)}, u32[]{:S(2)}) copy-start(bf16[512,256]{1,0:T(8,128)(2,1)} %get-tuple-element.41) | copy-start | bytes 786436
  40.9 2.3 %collective-permute-start.7 = (bf16[512,256]{1,0:T(8,128)(2,1)}, bf16[512,256]{1,0:T(8,128)(2,1)S(1)}, u32[]{:S(2)}, u32[]{:S(2)}) collective-permute-start(bf16[512,256]{1,0:T(8,128)(2,1)} %get-tuple-element.38), channel_id=1, source_target_pairs={{0,1},{1,0},{2,3},{3,2},{4,5},{5,4},{6,7},{7,6},{8,9},{9,8},{10,11... | collective-permute-start | bytes 786440 | tf_op jit(solution)/shard_map/ppermute | solution.py:215
  41.4 3.7 %collective-permute-start.9 = (bf16[512,256]{1,0:T(8,128)(2,1)}, bf16[512,256]{1,0:T(8,128)(2,1)S(1)}, u32[]{:S(2)}, u32[]{:S(2)}) collective-permute-start(bf16[512,256]{1,0:T(8,128)(2,1)} %get-tuple-element.40), channel_id=1, source_target_pairs={{0,1},{1,0},{2,3},{3,2},{4,5},{5,4},{6,7},{7,6},{8,9},{9,8},{10,11... | collective-permute-start | bytes 786440 | tf_op jit(solution)/shard_map/ppermute | solution.py:215
  41.4 11.1 %collective-permute-start.14 = (bf16[512,128]{1,0:T(8,128)(2,1)}, bf16[512,128]{1,0:T(8,128)(2,1)S(1)}, u32[]{:S(2)}, u32[]{:S(2)}) collective-permute-start(bf16[512,128]{1,0:T(8,128)(2,1)} %get-tuple-element.45), channel_id=1, source_target_pairs={{0,8},{8,0},{16,24},{24,16},{1,9},{9,1},{17,25},{25,17},{2,10},{10... | collective-permute-start | bytes 393224 | tf_op jit(solution)/shard_map/ppermute | solution.py:212
  42.6 5.1 %collective-permute-start.11 = (bf16[512,256]{1,0:T(8,128)(2,1)}, bf16[512,256]{1,0:T(8,128)(2,1)S(1)}, u32[]{:S(2)}, u32[]{:S(2)}) collective-permute-start(bf16[512,256]{1,0:T(8,128)(2,1)} %get-tuple-element.42), channel_id=1, source_target_pairs={{0,1},{1,0},{2,3},{3,2},{4,5},{5,4},{6,7},{7,6},{8,9},{9,8},{10,11... | collective-permute-start | bytes 786440 | tf_op jit(solution)/shard_map/ppermute | solution.py:215
  42.8 11.0 %collective-permute-start.13 = (bf16[512,256]{1,0:T(8,128)(2,1)}, bf16[512,256]{1,0:T(8,128)(2,1)S(1)}, u32[]{:S(2)}, u32[]{:S(2)}) collective-permute-start(bf16[512,256]{1,0:T(8,128)(2,1)} %get-tuple-element.44), channel_id=1, source_target_pairs={{0,1},{1,0},{2,3},{3,2},{4,5},{5,4},{6,7},{7,6},{8,9},{9,8},{10,11... | collective-permute-start | bytes 786440 | tf_op jit(solution)/shard_map/ppermute | solution.py:215
  44.1 21.5 %collective-permute-start.8 = (bf16[512,256]{1,0:T(8,128)(2,1)S(1)}, bf16[512,256]{1,0:T(8,128)(2,1)S(1)}, u32[]{:S(2)}, u32[]{:S(2)}) collective-permute-start(bf16[512,256]{1,0:T(8,128)(2,1)S(1)} %add_convert_fusion.2), channel_id=1, source_target_pairs={{0,8},{8,0},{16,24},{24,16},{1,9},{9,1},{17,25},{25,17},{2,10},{10... | collective-permute-start | bytes 786440 | tf_op jit(solution)/shard_map/ppermute | solution.py:212
  46.1 19.5 %collective-permute-start.10 = (bf16[512,256]{1,0:T(8,128)(2,1)S(1)}, bf16[512,256]{1,0:T(8,128)(2,1)S(1)}, u32[]{:S(2)}, u32[]{:S(2)}) collective-permute-start(bf16[512,256]{1,0:T(8,128)(2,1)S(1)} %add_convert_fusion.1), channel_id=1, source_target_pairs={{0,16},{8,24},{16,0},{24,8},{1,17},{9,25},{17,1},{25,9},{2,18},{10... | collective-permute-start | bytes 786440 | tf_op jit(solution)/shard_map/ppermute | solution.py:212
  47.7 17.9 %collective-permute-start.12 = (bf16[512,256]{1,0:T(8,128)(2,1)S(1)}, bf16[512,256]{1,0:T(8,128)(2,1)S(1)}, u32[]{:S(2)}, u32[]{:S(2)}) collective-permute-start(bf16[512,256]{1,0:T(8,128)(2,1)S(1)} %add_convert_fusion), channel_id=1, source_target_pairs={{0,24},{8,16},{16,8},{24,0},{1,25},{9,17},{17,9},{25,1},{2,26},{10... | collective-permute-start | bytes 786440 | tf_op jit(solution)/shard_map/ppermute | solution.py:212
  48.9 3.6 %copy-start.12 = (bf16[512,128]{1,0:T(8,128)(2,1)S(1)}, bf16[512,128]{1,0:T(8,128)(2,1)}, u32[]{:S(2)}) copy-start(bf16[512,128]{1,0:T(8,128)(2,1)} %get-tuple-element.46) | copy-start | bytes 393220
  48.9 4.8 %copy-start.11 = (bf16[512,128]{1,0:T(8,128)(2,1)S(1)}, bf16[512,128]{1,0:T(8,128)(2,1)}, u32[]{:S(2)}) copy-start(bf16[512,128]{1,0:T(8,128)(2,1)} %get-tuple-element.47) | copy-start | bytes 393220
  48.9 6.0 %copy-start.10 = (bf16[512,256]{1,0:T(8,128)(2,1)S(1)}, bf16[512,256]{1,0:T(8,128)(2,1)}, u32[]{:S(2)}) copy-start(bf16[512,256]{1,0:T(8,128)(2,1)} %get-tuple-element.43) | copy-start | bytes 786436
  52.5 13.1 %collective-permute-start.15 = (bf16[512,128]{1,0:T(8,128)(2,1)S(1)}, bf16[512,128]{1,0:T(8,128)(2,1)S(1)}, u32[]{:S(2)}, u32[]{:S(2)}) collective-permute-start(bf16[512,128]{1,0:T(8,128)(2,1)S(1)} %copy-done.12), channel_id=1, source_target_pairs={{0,16},{8,24},{16,0},{24,8},{1,17},{9,25},{17,1},{25,9},{2,18},{10... | collective-permute-start | bytes 393224 | tf_op jit(solution)/shard_map/ppermute | solution.py:212
  53.8 11.8 %collective-permute-start.16 = (bf16[512,128]{1,0:T(8,128)(2,1)S(1)}, bf16[512,128]{1,0:T(8,128)(2,1)S(1)}, u32[]{:S(2)}, u32[]{:S(2)}) collective-permute-start(bf16[512,128]{1,0:T(8,128)(2,1)S(1)} %copy-done.11), channel_id=1, source_target_pairs={{0,24},{8,16},{16,8},{24,0},{1,25},{9,17},{17,9},{25,1},{2,26},{10... | collective-permute-start | bytes 393224 | tf_op jit(solution)/shard_map/ppermute | solution.py:212
  65.9 7.3 %collective-permute-start.19 = (bf16[128,384]{1,0:T(8,128)(2,1)S(1)}, bf16[128,384]{1,0:T(8,128)(2,1)S(1)}, u32[]{:S(2)}, u32[]{:S(2)}) collective-permute-start(bf16[128,384]{1,0:T(8,128)(2,1)S(1)} %get-tuple-element.67), channel_id=1, source_target_pairs={{0,6},{1,7},{2,4},{3,5},{4,2},{5,3},{6,0},{7,1},{8,14},{9,15},{10,... | collective-permute-start | bytes 294920 | tf_op jit(solution)/shard_map/ppermute | solution.py:215
  69.6 8.2 %collective-permute-start.18 = (bf16[128,384]{1,0:T(8,128)(2,1)S(1)}, bf16[128,384]{1,0:T(8,128)(2,1)S(1)}, u32[]{:S(2)}, u32[]{:S(2)}) collective-permute-start(bf16[128,384]{1,0:T(8,128)(2,1)S(1)} %get-tuple-element.68), channel_id=1, source_target_pairs={{0,4},{1,5},{2,6},{3,7},{4,0},{5,1},{6,2},{7,3},{8,12},{9,13},{10,... | collective-permute-start | bytes 294920 | tf_op jit(solution)/shard_map/ppermute | solution.py:215
  69.6 8.2 %collective-permute-start.17 = (bf16[128,384]{1,0:T(8,128)(2,1)S(1)}, bf16[128,384]{1,0:T(8,128)(2,1)S(1)}, u32[]{:S(2)}, u32[]{:S(2)}) collective-permute-start(bf16[128,384]{1,0:T(8,128)(2,1)S(1)} %get-tuple-element.66), channel_id=1, source_target_pairs={{0,2},{1,3},{2,0},{3,1},{4,6},{5,7},{6,4},{7,5},{8,10},{9,11},{10,... | collective-permute-start | bytes 294920 | tf_op jit(solution)/shard_map/ppermute | solution.py:215
  77.8 10.2 %copy-start.7 = (bf16[128,384]{1,0:T(8,128)(2,1)}, bf16[128,384]{1,0:T(8,128)(2,1)S(1)}, u32[]{:S(2)}) copy-start(bf16[128,384]{1,0:T(8,128)(2,1)S(1)} %fusion.10.rest_0_) | copy-start | bytes 294916
  77.8 5.0 %collective-permute-start.20 = (bf16[128,384]{1,0:T(8,128)(2,1)S(1)}, bf16[128,384]{1,0:T(8,128)(2,1)S(1)}, u32[]{:S(2)}, u32[]{:S(2)}) collective-permute-start(bf16[128,384]{1,0:T(8,128)(2,1)S(1)} %fusion.10.rest_0_), channel_id=1, source_target_pairs={{0,2},{1,3},{2,0},{3,1},{4,6},{5,7},{6,4},{7,5},{8,10},{9,11},{10,... | collective-permute-start | bytes 294920 | tf_op jit(solution)/shard_map/ppermute | solution.py:215
  78.4 9.6 %collective-permute-start.21 = (bf16[128,384]{1,0:T(8,128)(2,1)S(1)}, bf16[128,384]{1,0:T(8,128)(2,1)S(1)}, u32[]{:S(2)}, u32[]{:S(2)}) collective-permute-start(bf16[128,384]{1,0:T(8,128)(2,1)S(1)} %fusion.10.rest_0_), channel_id=1, source_target_pairs={{0,4},{1,5},{2,6},{3,7},{4,0},{5,1},{6,2},{7,3},{8,12},{9,13},{10,... | collective-permute-start | bytes 294920 | tf_op jit(solution)/shard_map/ppermute | solution.py:215
  81.0 7.0 %collective-permute-start.22 = (bf16[128,384]{1,0:T(8,128)(2,1)S(1)}, bf16[128,384]{1,0:T(8,128)(2,1)S(1)}, u32[]{:S(2)}, u32[]{:S(2)}) collective-permute-start(bf16[128,384]{1,0:T(8,128)(2,1)S(1)} %fusion.10.rest_0_), channel_id=1, source_target_pairs={{0,6},{1,7},{2,4},{3,5},{4,2},{5,3},{6,0},{7,1},{8,14},{9,15},{10,... | collective-permute-start | bytes 294920 | tf_op jit(solution)/shard_map/ppermute | solution.py:215
  82.8 5.2 %copy-start.13 = (bf16[128,384]{1,0:T(8,128)(2,1)}, bf16[128,384]{1,0:T(8,128)(2,1)S(1)}, u32[]{:S(2)}) copy-start(bf16[128,384]{1,0:T(8,128)(2,1)S(1)} %collective-permute-done.20.rest_1_) | copy-start | bytes 294916
  88.0 0.6 copy-start.14
  88.7 0.6 copy-start.15
  91.2 7.7 %collective-permute-start.23 = (bf16[512,384]{1,0:T(8,128)(2,1)}, bf16[512,384]{1,0:T(8,128)(2,1)S(1)}, u32[]{:S(2)}, u32[]{:S(2)}) collective-permute-start(bf16[512,384]{1,0:T(8,128)(2,1)} %get-tuple-element.57.own), channel_id=1, source_target_pairs={{0,1},{1,0},{2,3},{3,2},{4,5},{5,4},{6,7},{7,6},{8,9},{9,8},{10,11... | collective-permute-start | bytes 1179656 | tf_op jit(solution)/shard_map/ppermute | solution.py:215
  91.2 3.7 %collective-permute-start.25 = (f32[1,128]{1,0:T(1,128)}, f32[1,128]{1,0:T(1,128)S(1)}, u32[]{:S(2)}, u32[]{:S(2)}) collective-permute-start(f32[1,128]{1,0:T(1,128)} %get-tuple-element.58), channel_id=1, source_target_pairs={{0,16},{8,24},{16,0},{24,8},{1,17},{9,25},{17,1},{25,9},{2,18},{10... | collective-permute-start | bytes 1544 | tf_op jit(solution)/shard_map/ppermute | solution.py:212
  91.9 4.6 %collective-permute-start.26 = (f32[1,128]{1,0:T(1,128)}, f32[1,128]{1,0:T(1,128)S(1)}, u32[]{:S(2)}, u32[]{:S(2)}) collective-permute-start(f32[1,128]{1,0:T(1,128)} %get-tuple-element.58), channel_id=1, source_target_pairs={{0,24},{8,16},{16,8},{24,0},{1,25},{9,17},{17,9},{25,1},{2,26},{10... | collective-permute-start | bytes 1544 | tf_op jit(solution)/shard_map/ppermute | solution.py:212
  93.3 3.7 %collective-permute-start.24 = (f32[1,128]{1,0:T(1,128)}, f32[1,128]{1,0:T(1,128)S(1)}, u32[]{:S(2)}, u32[]{:S(2)}) collective-permute-start(f32[1,128]{1,0:T(1,128)} %get-tuple-element.58), channel_id=1, source_target_pairs={{0,8},{8,0},{16,24},{24,16},{1,9},{9,1},{17,25},{25,17},{2,10},{10... | collective-permute-start | bytes 1544 | tf_op jit(solution)/shard_map/ppermute | solution.py:212
  97.7 1.2 %copy-start.17 = (f32[1,128]{1,0:T(1,128)}, f32[1,128]{1,0:T(1,128)S(1)}, u32[]{:S(2)}) copy-start(f32[1,128]{1,0:T(1,128)S(1)} %add_add_fusion.1.line) | copy-start | bytes 1540
  97.7 1.2 %collective-permute-start.27 = (f32[1,128]{1,0:T(1,128)S(1)}, f32[1,128]{1,0:T(1,128)S(1)}, u32[]{:S(2)}, u32[]{:S(2)}) collective-permute-start(f32[1,128]{1,0:T(1,128)S(1)} %add_add_fusion.1.line), channel_id=1, source_target_pairs={{0,1},{1,0},{2,3},{3,2},{4,5},{5,4},{6,7},{7,6},{8,9},{9,8},{10,11... | collective-permute-start | bytes 1544 | tf_op jit(solution)/shard_map/ppermute | solution.py:215
  98.9 0.6 copy-start.18
  99.5 0.8 copy-start.8
where the time goes:
time: 103 us
  waiting for transfers between devices  42.5 us (41%)
  starting transfers between devices  25.9 us (25%)
  Pallas kernels  19.3 us (19%)
  other arithmetic  8.1 us (8%)
  local copies, waits for them, and re-layouts  5.23 us (5%)
  between operations  1.53 us (1%)
    ppermute x12, waiting for transfers between devices, to_shard(): return lax.ppermute(value, 'fsdp', [(i, i ^ mask) for i in range(shards)])  28.2 us
    pallas_call x6, Pallas kernels, call(): pl.pallas_call(kernel, out_shape=outs, in_specs=[SMEM] + [VMEM] * len(arg...  19.3 us
    ppermute x12, starting transfers between devices, to_shard(): return lax.ppermute(value, 'fsdp', [(i, i ^ mask) for i in range(shards)])  14.8 us
    ppermute x16, waiting for transfers between devices, to_member(): return lax.ppermute(value, 'rep', [(i, i ^ mask) for i in range(copies)])  14.3 us
    ppermute x16, starting transfers between devices, to_member(): return lax.ppermute(value, 'rep', [(i, i ^ mask) for i in range(copies)])  11.1 us
    unnamed x41, local copies, waits for them, and re-layouts  4.41 us
    convert_element_type x3, other arithmetic, body(): qkv_got.append(to_shard(both.astype(bf16), mask) if mask else both)  2.1 us
  transfers between devices with their start and end apart: 28, of which 11 were waited for; matrix products, arithmetic and copies ran while one was open for 9% of the time, Pallas kernels for 5%

commit v1 on v0

--- a/solution.py
+++ b/solution.py
@@ -12,6 +12,7 @@
 
 
 VMEM = pl.BlockSpec(memory_space=pltpu.VMEM)
+ANY = pl.BlockSpec(memory_space=pl.ANY)
 SMEM = pl.BlockSpec(memory_space=pltpu.SMEM)
 
 
@@ -45,7 +46,8 @@
     out[:, half:] = w_out[:, half_cols(info[1], ohalf)]
 
 
-def out_terms_kernel(shards, info, out_grad, saved, keep, send):
+def out_terms_kernel(shards, info, out_grad, saved, *rest):
+    keep, send = rest[-2:]
     width = out_grad.shape[1] // shards
     half = saved.shape[1] // 2
     index, core = info[0], info[1]
@@ -134,33 +136,35 @@
         out[:, shard_cols(index, mask, width)] = total.astype(out.dtype)
 
 
-def gather_kernel(info, *rest):
-    pieces, own, square = rest[:-2], rest[-2], rest[-1]
-    rows = pieces[0].shape[0]
-    for mask, piece in enumerate(pieces):
-        spot = jnp.bitwise_xor(info[2], mask) * rows
-        own[pl.ds(pl.multiple_of(spot, rows), rows), :] = piece[...]
-    total = jnp.sum(jnp.square(own[...].astype(jnp.float32)))
-    square[...] = jnp.full(square.shape, total, jnp.float32)
-
-
-def finish_kernel(count, half, info, own, other, line, away, out, norm):
+def pack_kernel(mask, info, keep, arrived, part, out):
+    rows, ohalf = keep.shape[0], part.shape[2]
+    mid = part.shape[1] // 2
+    total = keep[...].astype(jnp.float32) + arrived[...].astype(jnp.float32)
+    out[:rows] = total.astype(out.dtype)
+    out[rows:, :ohalf] = part[mask, :mid].astype(out.dtype)
+    out[rows:, ohalf:] = part[mask, mid:].astype(out.dtype)
+
+
+def finish_kernel(count, half, info, line, away, *rest):
+    pieces, out, norm = rest[:-2], rest[-2], rest[-1]
     norm_sq = line[...] + away[...]
     scale = lax.rsqrt(norm_sq / count + 1e-06)
     norm[...] = jnp.sqrt(norm_sq)
-    ohalf = own.shape[1] - half
-    core, lanes = info[1], scale.shape[1]
-    for part, side in ((own, core), (other, 1 - core)):
-        for lower in range(0, half, lanes):
-            spot = pl.ds(pl.multiple_of(side * half + lower, lanes), lanes)
-            out[:, spot] = part[:, lower : lower + lanes].astype(jnp.float32) * scale
-        for lower in range(0, ohalf, lanes):
-            spot = pl.ds(pl.multiple_of(2 * half + side * ohalf + lower, lanes), lanes)
-            block = part[:, half + lower : half + lower + lanes]
-            out[:, spot] = block.astype(jnp.float32) * scale
-
-
-def vmem_call(kernel, outs, scratch=()):
+    number, (rows, columns) = len(pieces) // 2, pieces[0].shape
+    core, lanes, ohalf = info[1], scale.shape[1], columns - half
+    for which, piece in enumerate(pieces):
+        side = core if which < number else 1 - core
+        spot = slice(None)
+        if number > 1:
+            row = jnp.bitwise_xor(info[2], which % number) * rows
+            spot = pl.ds(pl.multiple_of(row, rows), rows)
+        for lower in range(0, columns, lanes):
+            start = side * half if lower < half else half + side * ohalf
+            cols = pl.ds(pl.multiple_of(start + lower, lanes), lanes)
+            out[spot, cols] = piece[:, lower : lower + lanes].astype(jnp.float32) * scale
+
+
+def vmem_call(kernel, outs, scratch=(), waits=0):
     def run(info, *args):
         return call(info, *args)
 
@@ -168,7 +172,7 @@
         return pl.pallas_call(
             kernel,
             out_shape=outs,
-            in_specs=[SMEM] + [VMEM] * len(args),
+            in_specs=[SMEM] + [VMEM] * (len(args) - waits) + [ANY] * waits,
             out_specs=jax.tree.map(lambda _: VMEM, outs),
             scratch_shapes=list(scratch),
         )(info, *args)
@@ -235,13 +239,21 @@
 
     out_shape = jax.ShapeDtypeStruct((shards, width, ohalf), bf16)
     out_keep, out_send = vmem_call(
-        functools.partial(out_terms_kernel, shards), [out_shape] * 2
-    )(info, out_grad, attn_saved)
+        functools.partial(out_terms_kernel, shards), [out_shape] * 2, waits=4
+    )(info, out_grad, attn_saved, cosine, sines, allowed, row_lse)
+    theirs = [to_member(chunk, 1) for chunk in mine]
+    piece_rows = width // groups
+
+    def reduce_groups(total, axis):
+        low = total.astype(bf16)
+        piece = lax.dynamic_slice_in_dim(total, place * piece_rows, piece_rows, axis)
+        for mask in range(1, groups):
+            away = lax.dynamic_slice_in_dim(low, (place ^ mask) * piece_rows, piece_rows, axis)
+            piece = piece + to_member(away, 2 * mask).astype(jnp.float32)
+        return piece
+
     out_sum = out_keep.astype(jnp.float32) + to_member(out_send, 1).astype(jnp.float32)
-    out_low = [out_sum[mask].astype(bf16) for mask in range(1, shards)]
-    out_low, fence = lax.optimization_barrier((out_low, mine))
-    theirs = [to_member(chunk, 1) for chunk in fence]
-    out_got = [to_shard(low, mask + 1) for mask, low in enumerate(out_low)]
+    out_part = reduce_groups(out_sum, 1)
 
     qkv_shape = jax.ShapeDtypeStruct((width, half), bf16)
     results = vmem_call(
@@ -252,49 +264,39 @@
             pltpu.VMEM((rows, w_out_t.shape[1]), jnp.float32),
         ],
     )(info, hidden_in, out_grad, attn_saved, row_lse, cosine, sines, allowed, w_qkv, w_out_t,
-      *fence, *theirs)
+      *mine, *theirs)
     d_qkv, keep, send = results[0], results[1 : shards + 1], results[shards + 1 :]
     input_grad = vmem_call(
         functools.partial(input_kernel, shards), jax.ShapeDtypeStruct(hidden_in.shape, bf16)
-    )(info, d_qkv, w_qkv, *fence, *theirs)
-
-    qkv_got = []
+    )(info, d_qkv, w_qkv, *mine, *theirs)
+
+    mid = piece_rows // 2
+    got = []
     for mask in list(range(1, shards)) + [0]:
-        both = keep[mask].astype(jnp.float32) + to_member(send[mask], 1).astype(jnp.float32)
-        qkv_got.append(to_shard(both.astype(bf16), mask) if mask else both)
-    qkv_got, out_got, input_grad = lax.optimization_barrier((qkv_got, out_got, input_grad))
-    total = jnp.concatenate(
-        [
-            sum(part.astype(jnp.float32) for part in qkv_got),
-            sum((part.astype(jnp.float32) for part in out_got), out_sum[0]),
-        ],
-        axis=1,
-    )
-    low = total.astype(bf16)
-    piece_rows = width // groups
-    piece = lax.dynamic_slice_in_dim(total, place * piece_rows, piece_rows, 0)
-    for mask in range(1, groups):
-        away = lax.dynamic_slice_in_dim(low, (place ^ mask) * piece_rows, piece_rows, 0)
-        piece = piece + to_member(away, 2 * mask).astype(jnp.float32)
+        kind = bf16 if mask else jnp.float32
+        both = vmem_call(
+            functools.partial(pack_kernel, mask), jax.ShapeDtypeStruct((width + mid, half), kind)
+        )(info, keep[mask], to_member(send[mask], 1), out_part)
+        got.append(to_shard(both, mask) if mask else both)
+    got, input_grad = lax.optimization_barrier((got, input_grad))
+    total = sum(part.astype(jnp.float32) for part in got)
+    out_piece = jnp.concatenate([total[width:, :ohalf], total[width:, ohalf:]], axis=0)
+    piece = jnp.concatenate([reduce_groups(total[:width], 0), out_piece], axis=1)
     low = piece.astype(bf16)
-    pieces = [low] + [to_member(low, 2 * mask) for mask in range(1, groups)]
+    square = jnp.full((1, 128), jnp.sum(jnp.square(piece)), jnp.float32)
+    own = [low] + [to_member(low, 2 * mask) for mask in range(1, groups)]
+    other = [to_member(part, 1) for part in own]
+    line = tree_sum([square] + [to_shard(square, mask) for mask in range(1, shards)])
+    line = tree_sum([line] + [to_member(line, 2 * mask) for mask in range(1, groups)])
+    away = to_member(line, 1)
+    if piece_rows % 16:
+        own, other = [arrange(own, place)], [arrange(other, place)]
     columns = half + ohalf
     line_shape = jax.ShapeDtypeStruct((1, 128), jnp.float32)
-    if piece_rows % 16 == 0:
-        own, square = vmem_call(
-            gather_kernel, [jax.ShapeDtypeStruct((width, columns), bf16), line_shape]
-        )(info, *pieces)
-    else:
-        own = arrange(pieces, place)
-        square = jnp.sum(jnp.square(own.astype(jnp.float32)))
-        square = jnp.full((1, 128), square, jnp.float32)
-    other = to_member(own, 1)
-    line = tree_sum([square] + [to_shard(square, mask) for mask in range(1, shards)])
-    away = to_member(line, 1)
     grad_update, norm = vmem_call(
         functools.partial(finish_kernel, float(width * shards * 2 * columns), half),
         [jax.ShapeDtypeStruct((width, 2 * columns), jnp.float32), line_shape],
-    )(info, own, other, line, away)
+    )(info, line, away, *own, *other)
     return (input_grad, grad_update, norm[0, 0])
 
 

time: 103 us -> 109 us (1.058)
  waiting for transfers between devices: 42.5 us -> 35.6 us
  Pallas kernels: 19.3 us -> 25.1 us
  local copies, waits for them, and re-layouts: 5.23 us -> 9.42 us
  starting transfers between devices: 25.9 us -> 28.1 us
  other arithmetic: 8.1 us -> 9.27 us
    ppermute x12 -> x9, waiting for transfers between devices: 28.2 us -> 19.2 us  [to_shard(): return lax.ppermute(value, 'fsdp', [(i, i ^ mask) for i in range(shards)])]
    ppermute x16 -> x25, starting transfers between devices: 11.1 us -> 17.1 us  [to_member(): return lax.ppermute(value, 'rep', [(i, i ^ mask) for i in range(copies)])]
    pallas_call x6 -> x9, Pallas kernels: 19.3 us -> 25.1 us  [call(): pl.pallas_call(kernel, out_shape=outs, in_specs=[SMEM] + [VMEM] * (len(ar...]
    ppermute x12 -> x9, starting transfers between devices: 14.8 us -> 11 us  [to_shard(): return lax.ppermute(value, 'fsdp', [(i, i ^ mask) for i in range(shards)])]
    unnamed x41 -> x45, local copies, waits for them, and re-layouts: 4.41 us -> 7.9 us
    add x3, other arithmetic: 0.22 us -> 2.86 us  [the longest x2 1.68 us: reduce_groups(): piece = piece + to_member(away, 2 * mask).astype(jnp.float32)]
    convert_element_type x4 -> x0, other arithmetic: 2.15 us -> none  [the longest x3 2.1 us: body(): qkv_got.append(to_shard(both.astype(bf16), mask) if mask else both)]
    ppermute x16 -> x25, waiting for transfers between devices: 14.3 us -> 16.4 us  [to_member(): return lax.ppermute(value, 'rep', [(i, i ^ mask) for i in range(copies)])]
  transfers between devices with their start and end apart: 28 -> 34, of which waited for: 11 -> 13; matrix products, arithmetic and copies ran while one was open for 9% -> 4% of each run, Pallas kernels for 5% -> 18%
where the time goes in v1:
time: 109 us
  waiting for transfers between devices  35.6 us (33%)
  starting transfers between devices  28.1 us (26%)
  Pallas kernels  25.1 us (23%)
  local copies, waits for them, and re-layouts  9.42 us (9%)
  other arithmetic  9.27 us (9%)
  between operations  1.55 us (1%)
    pallas_call x9, Pallas kernels, call(): pl.pallas_call(kernel, out_shape=outs, in_specs=[SMEM] + [VMEM] * (len(ar...  25.1 us
    ppermute x9, waiting for transfers between devices, to_shard(): return lax.ppermute(value, 'fsdp', [(i, i ^ mask) for i in range(shards)])  19.2 us
    ppermute x25, starting transfers between devices, to_member(): return lax.ppermute(value, 'rep', [(i, i ^ mask) for i in range(copies)])  17.1 us
    ppermute x25, waiting for transfers between devices, to_member(): return lax.ppermute(value, 'rep', [(i, i ^ mask) for i in range(copies)])  16.4 us
    ppermute x9, starting transfers between devices, to_shard(): return lax.ppermute(value, 'fsdp', [(i, i ^ mask) for i in range(shards)])  11 us
    unnamed x45, local copies, waits for them, and re-layouts  7.9 us
  transfers between devices with their start and end apart: 34, of which 13 were waited for; matrix products, arithmetic and copies ran while one was open for 4% of the time, Pallas kernels for 18%

profile of v1, /device:TPU:0, one launch (start us, length us, event | category | flops | bytes accessed | tf_op | source)
XLA Modules:
  0.0 109.0 jit_solution(8376573584557924411)
XLA Ops:
  1.3 0.8 reduce-window.8
  2.2 1.5 %copy.13.lse.rest_3_ = f32[256,2]{1,0:T(8,128)} copy(f32[256,2]{0,1:T(2,128)} %param.11) | data formatting | bytes 4096 | tf_op args[3]
  3.7 0.8 fusion.1.allowed.rest_2_
  5.0 0.7 pad_add_fusion.info
  5.7 0.8 pad_maximum_fusion
  6.5 3.0 %shard_map.105 = (bf16[4,512,128]{2,1,0:T(8,128)(2,1)}, bf16[4,512,128]{2,1,0:T(8,128)(2,1)}) custom-call(s32[3]{0:T(128)} %pad_add_fusion.info, bf16[256,2048]{1,0:T(8,128)(2,1)} %out_grad.3, bf16[256,256]{1,0:T(8,128)(2,1)} %saved.3, f32[256,128]{1,0:T(8,128)} %get-tuple-element.52.cosine.rest_0_, f32[256,128]{1,0:T(8,128)} %get-tuple-element.53.sines.rest_1_, ...), custom_call_target="tpu_custom_call" | custom-call | tf_op jit(solution)/shard_map/pallas_call | solution.py:172
  10.0 1.9 %shard_map.103 = bf16[512,384]{1,0:T(8,128)(2,1)} custom-call(s32[3]{0:T(128)} %pad_add_fusion.info, bf16[512,512]{1,0:T(8,128)(2,1)} %w_qkv.5, bf16[512,256]{1,0:T(8,128)(2,1)} %w_out.3), custom_call_target="tpu_custom_call" | custom-call | tf_op jit(solution)/shard_map/pallas_call | solution.py:172
  11.9 3.4 %collective-permute-start.2 = (bf16[512,384]{1,0:T(8,128)(2,1)}, bf16[512,384]{1,0:T(8,128)(2,1)S(1)}, u32[]{:S(2)}, u32[]{:S(2)}) collective-permute-start(bf16[512,384]{1,0:T(8,128)(2,1)} %shard_map.103), channel_id=1, source_target_pairs={{0,24},{8,16},{16,8},{24,0},{1,25},{9,17},{17,9},{25,1},{2,26},{10... | collective-permute-start | bytes 1179656 | tf_op jit(solution)/shard_map/ppermute | solution.py:216
  15.9 9.7 %collective-permute-done.2.rest_2_ = bf16[512,384]{1,0:T(8,128)(2,1)S(1)} collective-permute-done((bf16[512,384]{1,0:T(8,128)(2,1)}, bf16[512,384]{1,0:T(8,128)(2,1)S(1)}, u32[]{:S(2)}, u32[]{:S(2)}) %collective-permute-start.2) | collective-permute-done | bytes 393248 | tf_op jit(solution)/shard_map/ppermute | solution.py:216
  25.6 8.2 %collective-permute-done.1.rest_1_ = bf16[512,384]{1,0:T(8,128)(2,1)S(1)} collective-permute-done((bf16[512,384]{1,0:T(8,128)(2,1)}, bf16[512,384]{1,0:T(8,128)(2,1)S(1)}, u32[]{:S(2)}, u32[]{:S(2)}) %collective-permute-start.1) | collective-permute-done | bytes 393248 | tf_op jit(solution)/shard_map/ppermute | solution.py:216
  34.3 0.8 copy-done.6
  35.1 1.3 %convert_add_fusion = (f32[4,512,128]{2,1,0:T(8,128)S(1)}, bf16[4,512,128]{2,1,0:T(8,128)(2,1)S(1)}) fusion(bf16[4,512,128]{2,1,0:T(8,128)(2,1)} %copy-done.6, bf16[4,512,128]{2,1,0:T(8,128)(2,1)} %get-tuple-element.23), kind=kLoop, calls=%fused_computation | loop fusion | flops 1048576 | bytes 2621440 | tf_op jit(solution)/shard_map/add | solution.py:255
  36.4 0.8 constant_dynamic-slice_fusion.5
  37.2 1.8 %collective-permute-start.8 = (bf16[4,128,128]{2,1,0:T(8,128)(2,1)}, bf16[4,128,128]{2,1,0:T(8,128)(2,1)S(1)}, u32[]{:S(2)}, u32[]{:S(2)}) collective-permute-start(bf16[4,128,128]{2,1,0:T(8,128)(2,1)} %get-tuple-element.43), channel_id=1, source_target_pairs={{0,2},{1,3},{2,0},{3,1},{4,6},{5,7},{6,4},{7,5},{8,10},{9,11},{10,... | collective-permute-start | bytes 393224 | tf_op jit(solution)/shard_map/ppermute | solution.py:219
  39.0 2.5 %collective-permute-start.10 = (bf16[4,128,128]{2,1,0:T(8,128)(2,1)}, bf16[4,128,128]{2,1,0:T(8,128)(2,1)}, u32[]{:S(2)}, u32[]{:S(2)}) collective-permute-start(bf16[4,128,128]{2,1,0:T(8,128)(2,1)} %get-tuple-element.44), channel_id=1, source_target_pairs={{0,6},{1,7},{2,4},{3,5},{4,2},{5,3},{6,0},{7,1},{8,14},{9,15},{10,... | collective-permute-start | bytes 393224 | tf_op jit(solution)/shard_map/ppermute | solution.py:219
  42.5 0.7 copy-done.5
  43.2 6.5 %shard_map.104 = (bf16[256,512]{1,0:T(8,128)(2,1)}, bf16[512,256]{1,0:T(8,128)(2,1)}, bf16[512,256]{1,0:T(8,128)(2,1)}, bf16[512,256]{1,0:T(8,128)(2,1)}, bf16[5...) custom-call(s32[3]{0:T(128)} %pad_add_fusion.info, ...), custom_call_target="tpu_custom_call" | custom-call | tf_op jit(solution)/shard_map/pallas_call | solution.py:172
  50.3 3.5 %collective-permute-done.9 = bf16[4,128,128]{2,1,0:T(8,128)(2,1)S(1)} collective-permute-done((bf16[4,128,128]{2,1,0:T(8,128)(2,1)}, bf16[4,128,128]{2,1,0:T(8,128)(2,1)S(1)}, u32[]{:S(2)}, u32[]{:S(2)}) %collective-permute-start.9) | collective-permute-done | bytes 131104 | tf_op jit(solution)/shard_map/ppermute | solution.py:219
  53.8 1.6 %convert_add_fusion.1.part = f32[4,128,128]{2,1,0:T(8,128)} fusion(bf16[4,128,128]{2,1,0:T(8,128)(2,1)} %collective-permute-done.10, bf16[4,128,128]{2,1,0:T(8,128)(2,1)S(1)} %collective-permute-done.9, bf16[4,128,128]{2,1,0:T(8,128)(2,1)S(1)} %collective-permute-done.8, f32[4,512,128]{2,1,0:T(8,128)S(1)} %get-tuple-element.39, s32[]{:T(128)S(6)} %select_n.29), kind=kLoop, calls=%fused_computation.2 | loop fusion | flops 393216 | bytes 917508 | tf_op jit(solution)/shard_map/add | solution.py:252
  55.4 0.7 copy-done.11
  56.1 1.9 %shard_map.108 = bf16[576,256]{1,0:T(8,128)(2,1)} custom-call(s32[3]{0:T(128)} %pad_add_fusion.info, bf16[512,256]{1,0:T(8,128)(2,1)} %get-tuple-element.27.keep, bf16[512,256]{1,0:T(8,128)(2,1)} %copy-done.11, f32[4,128,128]{2,1,0:T(8,128)} %convert_add_fusion.1.part), custom_call_target="tpu_custom_call" | custom-call | tf_op jit(solution)/shard_map/pallas_call | solution.py:172
  58.1 1.7 %collective-permute-start.15 = (bf16[576,256]{1,0:T(8,128)(2,1)}, bf16[576,256]{1,0:T(8,128)(2,1)S(1)}, u32[]{:S(2)}, u32[]{:S(2)}) collective-permute-start(bf16[576,256]{1,0:T(8,128)(2,1)} %shard_map.108), channel_id=1, source_target_pairs={{0,24},{8,16},{16,8},{24,0},{1,25},{9,17},{17,9},{25,1},{2,26},{10... | collective-permute-start | bytes 884744 | tf_op jit(solution)/shard_map/ppermute | solution.py:216
  59.8 0.7 copy-done.10
  60.5 1.9 %shard_map.107 = bf16[576,256]{1,0:T(8,128)(2,1)} custom-call(s32[3]{0:T(128)} %pad_add_fusion.info, bf16[512,256]{1,0:T(8,128)(2,1)} %get-tuple-element.25.keep, bf16[512,256]{1,0:T(8,128)(2,1)} %copy-done.10, f32[4,128,128]{2,1,0:T(8,128)} %convert_add_fusion.1.part), custom_call_target="tpu_custom_call" | custom-call | tf_op jit(solution)/shard_map/pallas_call | solution.py:172
  62.4 1.2 %collective-permute-start.13 = (bf16[576,256]{1,0:T(8,128)(2,1)}, bf16[576,256]{1,0:T(8,128)(2,1)S(1)}, u32[]{:S(2)}, u32[]{:S(2)}) collective-permute-start(bf16[576,256]{1,0:T(8,128)(2,1)} %shard_map.107), channel_id=1, source_target_pairs={{0,16},{8,24},{16,0},{24,8},{1,17},{9,25},{17,1},{25,9},{2,18},{10... | collective-permute-start | bytes 884744 | tf_op jit(solution)/shard_map/ppermute | solution.py:216
  63.7 0.7 copy-done.9
  64.4 1.9 %shard_map.106 = bf16[576,256]{1,0:T(8,128)(2,1)} custom-call(s32[3]{0:T(128)} %pad_add_fusion.info, bf16[512,256]{1,0:T(8,128)(2,1)} %get-tuple-element.21.keep, bf16[512,256]{1,0:T(8,128)(2,1)} %copy-done.9, f32[4,128,128]{2,1,0:T(8,128)} %convert_add_fusion.1.part), custom_call_target="tpu_custom_call" | custom-call | tf_op jit(solution)/shard_map/pallas_call | solution.py:172
  66.8 3.6 %shard_map.110 = bf16[256,2048]{1,0:T(8,128)(2,1)} custom-call(s32[3]{0:T(128)} %pad_add_fusion.info, bf16[256,512]{1,0:T(8,128)(2,1)} %get-tuple-element.31.d_qkv, bf16[512,512]{1,0:T(8,128)(2,1)} %w_qkv.5, bf16[512,384]{1,0:T(8,128)(2,1)} %copy-done.2, bf16[512,384]{1,0:T(8,128)(2,1)} %copy-done.1, bf16[512,384]{1,0:T(8,128)(2,1)} %copy-done, ...), custom_call_target="tpu_custom_call" | custom-call | tf_op jit(solution)/shard_map/pallas_call | solution.py:172
  70.4 0.7 copy-done.8
  71.1 2.0 %shard_map.109 = f32[576,256]{1,0:T(8,128)} custom-call(s32[3]{0:T(128)} %pad_add_fusion.info, bf16[512,256]{1,0:T(8,128)(2,1)} %get-tuple-element.29.keep, bf16[512,256]{1,0:T(8,128)(2,1)} %copy-done.8, f32[4,128,128]{2,1,0:T(8,128)} %convert_add_fusion.1.part), custom_call_target="tpu_custom_call" | custom-call | tf_op jit(solution)/shard_map/pallas_call | solution.py:172
  73.1 0.7 collective-permute-done.13
  74.2 1.2 %add_add_fusion = f32[576,256]{1,0:T(8,128)S(1)} fusion(f32[576,256]{1,0:T(8,128)} %shard_map.109, bf16[576,256]{1,0:T(8,128)(2,1)S(1)} %collective-permute-done.15, bf16[576,256]{1,0:T(8,128)(2,1)S(1)} %collective-permute-done.13, bf16[576,256]{1,0:T(8,128)(2,1)S(1)} %collective-permute-done.11), kind=kLoop, calls=%fused_computation.1 | loop fusion | flops 884736 | bytes 2064384 | tf_op jit(solution)/shard_map/add | solution.py:282
  75.5 2.5 %collective-permute-start.19 = (bf16[128,256]{1,0:T(8,128)(2,1)S(1)}, bf16[128,256]{1,0:T(8,128)(2,1)S(1)}, u32[]{:S(2)}, u32[]{:S(2)}) collective-permute-start(bf16[128,256]{1,0:T(8,128)(2,1)S(1)} %get-tuple-element.47), channel_id=1, source_target_pairs={{0,6},{1,7},{2,4},{3,5},{4,2},{5,3},{6,0},{7,1},{8,14},{9,15},{10,... | collective-permute-start | bytes 196616 | tf_op jit(solution)/shard_map/ppermute | solution.py:219
  78.0 1.0 collective-permute-start.18
  79.0 0.9 collective-permute-done.17
  79.9 2.3 %collective-permute-done.19 = bf16[128,256]{1,0:T(8,128)(2,1)S(1)} collective-permute-done((bf16[128,256]{1,0:T(8,128)(2,1)S(1)}, bf16[128,256]{1,0:T(8,128)(2,1)S(1)}, u32[]{:S(2)}, u32[]{:S(2)}) %collective-permute-start.19) | collective-permute-done | bytes 65568 | tf_op jit(solution)/shard_map/ppermute | solution.py:219
  82.3 2.7 %collective-permute-done.18 = bf16[128,256]{1,0:T(8,128)(2,1)S(1)} collective-permute-done((bf16[128,256]{1,0:T(8,128)(2,1)S(1)}, bf16[128,256]{1,0:T(8,128)(2,1)S(1)}, u32[]{:S(2)}, u32[]{:S(2)}) %collective-permute-start.18) | collective-permute-done | bytes 65568 | tf_op jit(solution)/shard_map/ppermute | solution.py:219
  86.3 1.4 %collective-permute-start.21 = (f32[1,128]{1,0:T(1,128)S(1)}, f32[1,128]{1,0:T(1,128)S(1)}, u32[]{:S(2)}, u32[]{:S(2)}) collective-permute-start(f32[1,128]{1,0:T(1,128)S(1)} %broadcast_in_dim.2), channel_id=1, source_target_pairs={{0,16},{8,24},{16,0},{24,8},{1,17},{9,25},{17,1},{25,9},{2,18},{10... | collective-permute-start | bytes 1544 | tf_op jit(solution)/shard_map/ppermute | solution.py:216
  87.7 1.4 %collective-permute-start.22 = (f32[1,128]{1,0:T(1,128)S(1)}, f32[1,128]{1,0:T(1,128)S(1)}, u32[]{:S(2)}, u32[]{:S(2)}) collective-permute-start(f32[1,128]{1,0:T(1,128)S(1)} %broadcast_in_dim.2), channel_id=1, source_target_pairs={{0,24},{8,16},{16,8},{24,0},{1,25},{9,17},{17,9},{25,1},{2,26},{10... | collective-permute-start | bytes 1544 | tf_op jit(solution)/shard_map/ppermute | solution.py:216
  89.1 0.8 collective-permute-start.20
  89.9 2.1 %collective-permute-start.29 = (bf16[128,384]{1,0:T(8,128)(2,1)S(1)}, bf16[128,384]{1,0:T(8,128)(2,1)S(1)}, u32[]{:S(2)}, u32[]{:S(2)}) collective-permute-start(bf16[128,384]{1,0:T(8,128)(2,1)S(1)} %fusion.2.rest_0_), channel_id=1, source_target_pairs={{0,6},{1,7},{2,4},{3,5},{4,2},{5,3},{6,0},{7,1},{8,14},{9,15},{10,... | collective-permute-start | bytes 294920 | tf_op jit(solution)/shard_map/ppermute | solution.py:219
  91.9 2.4 %collective-permute-start.27 = (bf16[128,384]{1,0:T(8,128)(2,1)S(1)}, bf16[128,384]{1,0:T(8,128)(2,1)S(1)}, u32[]{:S(2)}, u32[]{:S(2)}) collective-permute-start(bf16[128,384]{1,0:T(8,128)(2,1)S(1)} %fusion.2.rest_0_), channel_id=1, source_target_pairs={{0,2},{1,3},{2,0},{3,1},{4,6},{5,7},{6,4},{7,5},{8,10},{9,11},{10,... | collective-permute-start | bytes 294920 | tf_op jit(solution)/shard_map/ppermute | solution.py:219
  95.0 2.1 %collective-permute-start.25 = (f32[1,128]{1,0:T(1,128)S(1)}, f32[1,128]{1,0:T(1,128)S(1)}, u32[]{:S(2)}, u32[]{:S(2)}) collective-permute-start(f32[1,128]{1,0:T(1,128)S(1)} %add_add_fusion.2), channel_id=1, source_target_pairs={{0,6},{1,7},{2,4},{3,5},{4,2},{5,3},{6,0},{7,1},{8,14},{9,15},{10,... | collective-permute-start | bytes 1544 | tf_op jit(solution)/shard_map/ppermute | solution.py:219
  97.1 3.4 %collective-permute-done.25 = f32[1,128]{1,0:T(1,128)S(1)} collective-permute-done((f32[1,128]{1,0:T(1,128)S(1)}, f32[1,128]{1,0:T(1,128)S(1)}, u32[]{:S(2)}, u32[]{:S(2)}) %collective-permute-start.25) | collective-permute-done | bytes 544 | tf_op jit(solution)/shard_map/ppermute | solution.py:219
  100.6 0.9 collective-permute-done.24
  102.6 1.4 %collective-permute-done.23 = f32[1,128]{1,0:T(1,128)S(1)} collective-permute-done((f32[1,128]{1,0:T(1,128)S(1)}, f32[1,128]{1,0:T(1,128)S(1)}, u32[]{:S(2)}, u32[]{:S(2)}) %collective-permute-start.23) | collective-permute-done | bytes 544 | tf_op jit(solution)/shard_map/ppermute | solution.py:219
  104.0 1.2 %collective-permute-done.26.away = f32[1,128]{1,0:T(1,128)S(1)} collective-permute-done((f32[1,128]{1,0:T(1,128)S(1)}, f32[1,128]{1,0:T(1,128)S(1)}, u32[]{:S(2)}, u32[]{:S(2)}) %collective-permute-start.26) | collective-permute-done | bytes 544 | tf_op jit(solution)/shard_map/ppermute | solution.py:219
  106.5 2.5 %shard_map.111 = (f32[512,768]{1,0:T(8,128)}, f32[1,128]{1,0:T(1,128)}) custom-call(s32[3]{0:T(128)} %pad_add_fusion.info, f32[1,128]{1,0:T(1,128)} %copy-done.19, f32[1,128]{1,0:T(1,128)} %copy-done.20, bf16[128,384]{1,0:T(8,128)(2,1)} %copy-done.7, bf16[128,384]{1,0:T(8,128)(2,1)} %copy-done.14, bf16[128,384]{1,0:T(8,128)(2,1)} %copy-done.13, ...), custom_call_target="tpu_custom_call" | custom-call | tf_op jit(solution)/shard_map/pallas_call | solution.py:172
  (96 shorter events, 9.4 us)
Async XLA Ops:
  9.5 24.8 %collective-permute-start.7 = (bf16[4,512,128]{2,1,0:T(8,128)(2,1)}, bf16[4,512,128]{2,1,0:T(8,128)(2,1)S(1)}, u32[]{:S(2)}, u32[]{:S(2)}) collective-permute-start(bf16[4,512,128]{2,1,0:T(8,128)(2,1)} %get-tuple-element.24), channel_id=1, source_target_pairs={{0,1},{1,0},{2,3},{3,2},{4,5},{5,4},{6,7},{7,6},{8,9},{9,8},{10,11... | collective-permute-start | bytes 1572872 | tf_op jit(solution)/shard_map/ppermute | solution.py:219
  11.9 13.7 %collective-permute-start.2 = (bf16[512,384]{1,0:T(8,128)(2,1)}, bf16[512,384]{1,0:T(8,128)(2,1)S(1)}, u32[]{:S(2)}, u32[]{:S(2)}) collective-permute-start(bf16[512,384]{1,0:T(8,128)(2,1)} %shard_map.103), channel_id=1, source_target_pairs={{0,24},{8,16},{16,8},{24,0},{1,25},{9,17},{17,9},{25,1},{2,26},{10... | collective-permute-start | bytes 1179656 | tf_op jit(solution)/shard_map/ppermute | solution.py:216
  15.3 18.4 %collective-permute-start.1 = (bf16[512,384]{1,0:T(8,128)(2,1)}, bf16[512,384]{1,0:T(8,128)(2,1)S(1)}, u32[]{:S(2)}, u32[]{:S(2)}) collective-permute-start(bf16[512,384]{1,0:T(8,128)(2,1)} %shard_map.103), channel_id=1, source_target_pairs={{0,16},{8,24},{16,0},{24,8},{1,17},{9,25},{17,1},{25,9},{2,18},{10... | collective-permute-start | bytes 1179656 | tf_op jit(solution)/shard_map/ppermute | solution.py:216
  15.8 18.2 %collective-permute-start = (bf16[512,384]{1,0:T(8,128)(2,1)}, bf16[512,384]{1,0:T(8,128)(2,1)S(1)}, u32[]{:S(2)}, u32[]{:S(2)}) collective-permute-start(bf16[512,384]{1,0:T(8,128)(2,1)} %shard_map.103), channel_id=1, source_target_pairs={{0,8},{8,0},{16,24},{24,16},{1,9},{9,1},{17,25},{25,17},{2,10},{10... | collective-permute-start | bytes 1179656 | tf_op jit(solution)/shard_map/ppermute | solution.py:216
  25.6 11.7 %copy-start = (bf16[512,384]{1,0:T(8,128)(2,1)}, bf16[512,384]{1,0:T(8,128)(2,1)S(1)}, u32[]{:S(2)}) copy-start(bf16[512,384]{1,0:T(8,128)(2,1)S(1)} %collective-permute-done.2.rest_2_) | copy-start | bytes 1179652
  25.6 16.0 %collective-permute-start.5 = (bf16[512,384]{1,0:T(8,128)(2,1)S(1)}, bf16[512,384]{1,0:T(8,128)(2,1)S(1)}, u32[]{:S(2)}, u32[]{:S(2)}) collective-permute-start(bf16[512,384]{1,0:T(8,128)(2,1)S(1)} %collective-permute-done.2.rest_2_), channel_id=1, source_target_pairs={{0,1},{1,0},{2,3},{3,2},{4,5},{5,4},{6,7},{7,6},{8,9},{9,8},{10,11... | collective-permute-start | bytes 1179656 | tf_op jit(solution)/shard_map/ppermute | solution.py:219
  33.8 3.5 %copy-start.1 = (bf16[512,384]{1,0:T(8,128)(2,1)}, bf16[512,384]{1,0:T(8,128)(2,1)S(1)}, u32[]{:S(2)}) copy-start(bf16[512,384]{1,0:T(8,128)(2,1)S(1)} %collective-permute-done.1.rest_1_) | copy-start | bytes 1179652
  33.8 8.0 %collective-permute-start.4 = (bf16[512,384]{1,0:T(8,128)(2,1)S(1)}, bf16[512,384]{1,0:T(8,128)(2,1)S(1)}, u32[]{:S(2)}, u32[]{:S(2)}) collective-permute-start(bf16[512,384]{1,0:T(8,128)(2,1)S(1)} %collective-permute-done.1.rest_1_), channel_id=1, source_target_pairs={{0,1},{1,0},{2,3},{3,2},{4,5},{5,4},{6,7},{7,6},{8,9},{9,8},{10,11... | collective-permute-start | bytes 1179656 | tf_op jit(solution)/shard_map/ppermute | solution.py:219
  34.0 3.2 %copy-start.2 = (bf16[512,384]{1,0:T(8,128)(2,1)}, bf16[512,384]{1,0:T(8,128)(2,1)S(1)}, u32[]{:S(2)}) copy-start(bf16[512,384]{1,0:T(8,128)(2,1)S(1)} %collective-permute-done.rest_0_) | copy-start | bytes 1179652
  34.0 7.7 %collective-permute-start.3 = (bf16[512,384]{1,0:T(8,128)(2,1)S(1)}, bf16[512,384]{1,0:T(8,128)(2,1)S(1)}, u32[]{:S(2)}, u32[]{:S(2)}) collective-permute-start(bf16[512,384]{1,0:T(8,128)(2,1)S(1)} %collective-permute-done.rest_0_), channel_id=1, source_target_pairs={{0,1},{1,0},{2,3},{3,2},{4,5},{5,4},{6,7},{7,6},{8,9},{9,8},{10,11... | collective-permute-start | bytes 1179656 | tf_op jit(solution)/shard_map/ppermute | solution.py:219
  34.3 0.8 copy-start.6
  37.2 13.0 %collective-permute-start.8 = (bf16[4,128,128]{2,1,0:T(8,128)(2,1)}, bf16[4,128,128]{2,1,0:T(8,128)(2,1)S(1)}, u32[]{:S(2)}, u32[]{:S(2)}) collective-permute-start(bf16[4,128,128]{2,1,0:T(8,128)(2,1)} %get-tuple-element.43), channel_id=1, source_target_pairs={{0,2},{1,3},{2,0},{3,1},{4,6},{5,7},{6,4},{7,5},{8,10},{9,11},{10,... | collective-permute-start | bytes 393224 | tf_op jit(solution)/shard_map/ppermute | solution.py:219
  39.0 11.3 %collective-permute-start.10 = (bf16[4,128,128]{2,1,0:T(8,128)(2,1)}, bf16[4,128,128]{2,1,0:T(8,128)(2,1)}, u32[]{:S(2)}, u32[]{:S(2)}) collective-permute-start(bf16[4,128,128]{2,1,0:T(8,128)(2,1)} %get-tuple-element.44), channel_id=1, source_target_pairs={{0,6},{1,7},{2,4},{3,5},{4,2},{5,3},{6,0},{7,1},{8,14},{9,15},{10,... | collective-permute-start | bytes 393224 | tf_op jit(solution)/shard_map/ppermute | solution.py:219
  41.5 0.8 copy-start.3
  41.5 12.2 %collective-permute-start.9 = (bf16[4,128,128]{2,1,0:T(8,128)(2,1)}, bf16[4,128,128]{2,1,0:T(8,128)(2,1)S(1)}, u32[]{:S(2)}, u32[]{:S(2)}) collective-permute-start(bf16[4,128,128]{2,1,0:T(8,128)(2,1)} %get-tuple-element.45), channel_id=1, source_target_pairs={{0,4},{1,5},{2,6},{3,7},{4,0},{5,1},{6,2},{7,3},{8,12},{9,13},{10,... | collective-permute-start | bytes 393224 | tf_op jit(solution)/shard_map/ppermute | solution.py:219
  41.7 0.8 copy-start.4
  42.5 0.7 copy-start.5
  49.7 5.7 %collective-permute-start.14 = (bf16[512,256]{1,0:T(8,128)(2,1)}, bf16[512,256]{1,0:T(8,128)(2,1)S(1)}, u32[]{:S(2)}, u32[]{:S(2)}) collective-permute-start(bf16[512,256]{1,0:T(8,128)(2,1)} %get-tuple-element.28), channel_id=1, source_target_pairs={{0,1},{1,0},{2,3},{3,2},{4,5},{5,4},{6,7},{7,6},{8,9},{9,8},{10,11... | collective-permute-start | bytes 786440 | tf_op jit(solution)/shard_map/ppermute | solution.py:219
  49.7 10.1 %collective-permute-start.12 = (bf16[512,256]{1,0:T(8,128)(2,1)}, bf16[512,256]{1,0:T(8,128)(2,1)S(1)}, u32[]{:S(2)}, u32[]{:S(2)}) collective-permute-start(bf16[512,256]{1,0:T(8,128)(2,1)} %get-tuple-element.26), channel_id=1, source_target_pairs={{0,1},{1,0},{2,3},{3,2},{4,5},{5,4},{6,7},{7,6},{8,9},{9,8},{10,11... | collective-permute-start | bytes 786440 | tf_op jit(solution)/shard_map/ppermute | solution.py:219
  50.2 13.4 %collective-permute-start.6 = (bf16[512,256]{1,0:T(8,128)(2,1)}, bf16[512,256]{1,0:T(8,128)(2,1)S(1)}, u32[]{:S(2)}, u32[]{:S(2)}) collective-permute-start(bf16[512,256]{1,0:T(8,128)(2,1)} %get-tuple-element.22), channel_id=1, source_target_pairs={{0,1},{1,0},{2,3},{3,2},{4,5},{5,4},{6,7},{7,6},{8,9},{9,8},{10,11... | collective-permute-start | bytes 786440 | tf_op jit(solution)/shard_map/ppermute | solution.py:219
  56.1 10.7 %copy-start.21 = (bf16[512,256]{1,0:T(8,128)(2,1)S(1)}, bf16[512,256]{1,0:T(8,128)(2,1)}, u32[]{:S(2)}) copy-start(bf16[512,256]{1,0:T(8,128)(2,1)} %get-tuple-element.30) | copy-start | bytes 786436
  58.1 15.0 %collective-permute-start.15 = (bf16[576,256]{1,0:T(8,128)(2,1)}, bf16[576,256]{1,0:T(8,128)(2,1)S(1)}, u32[]{:S(2)}, u32[]{:S(2)}) collective-permute-start(bf16[576,256]{1,0:T(8,128)(2,1)} %shard_map.108), channel_id=1, source_target_pairs={{0,24},{8,16},{16,8},{24,0},{1,25},{9,17},{17,9},{25,1},{2,26},{10... | collective-permute-start | bytes 884744 | tf_op jit(solution)/shard_map/ppermute | solution.py:216
  62.4 11.3 %collective-permute-start.13 = (bf16[576,256]{1,0:T(8,128)(2,1)}, bf16[576,256]{1,0:T(8,128)(2,1)S(1)}, u32[]{:S(2)}, u32[]{:S(2)}) collective-permute-start(bf16[576,256]{1,0:T(8,128)(2,1)} %shard_map.107), channel_id=1, source_target_pairs={{0,16},{8,24},{16,0},{24,8},{1,17},{9,25},{17,1},{25,9},{2,18},{10... | collective-permute-start | bytes 884744 | tf_op jit(solution)/shard_map/ppermute | solution.py:216
  63.7 0.7 copy-start.9
  66.3 7.9 %collective-permute-start.11 = (bf16[576,256]{1,0:T(8,128)(2,1)}, bf16[576,256]{1,0:T(8,128)(2,1)S(1)}, u32[]{:S(2)}, u32[]{:S(2)}) collective-permute-start(bf16[576,256]{1,0:T(8,128)(2,1)} %shard_map.106), channel_id=1, source_target_pairs={{0,8},{8,0},{16,24},{24,16},{1,9},{9,1},{17,25},{25,17},{2,10},{10... | collective-permute-start | bytes 884744 | tf_op jit(solution)/shard_map/ppermute | solution.py:216
  66.8 3.6 %collective-permute-start.16 = (bf16[512,256]{1,0:T(8,128)(2,1)S(1)}, bf16[512,256]{1,0:T(8,128)(2,1)S(1)}, u32[]{:S(2)}, u32[]{:S(2)}) collective-permute-start(bf16[512,256]{1,0:T(8,128)(2,1)S(1)} %copy-done.21), channel_id=1, source_target_pairs={{0,1},{1,0},{2,3},{3,2},{4,5},{5,4},{6,7},{7,6},{8,9},{9,8},{10,11... | collective-permute-start | bytes 786440 | tf_op jit(solution)/shard_map/ppermute | solution.py:219
  75.4 4.5 %collective-permute-start.17 = (bf16[128,256]{1,0:T(8,128)(2,1)S(1)}, bf16[128,256]{1,0:T(8,128)(2,1)S(1)}, u32[]{:S(2)}, u32[]{:S(2)}) collective-permute-start(bf16[128,256]{1,0:T(8,128)(2,1)S(1)} %get-tuple-element.46), channel_id=1, source_target_pairs={{0,2},{1,3},{2,0},{3,1},{4,6},{5,7},{6,4},{7,5},{8,10},{9,11},{10,... | collective-permute-start | bytes 196616 | tf_op jit(solution)/shard_map/ppermute | solution.py:219
  75.5 6.8 %collective-permute-start.19 = (bf16[128,256]{1,0:T(8,128)(2,1)S(1)}, bf16[128,256]{1,0:T(8,128)(2,1)S(1)}, u32[]{:S(2)}, u32[]{:S(2)}) collective-permute-start(bf16[128,256]{1,0:T(8,128)(2,1)S(1)} %get-tuple-element.47), channel_id=1, source_target_pairs={{0,6},{1,7},{2,4},{3,5},{4,2},{5,3},{6,0},{7,1},{8,14},{9,15},{10,... | collective-permute-start | bytes 196616 | tf_op jit(solution)/shard_map/ppermute | solution.py:219
  78.0 6.9 %collective-permute-start.18 = (bf16[128,256]{1,0:T(8,128)(2,1)S(1)}, bf16[128,256]{1,0:T(8,128)(2,1)S(1)}, u32[]{:S(2)}, u32[]{:S(2)}) collective-permute-start(bf16[128,256]{1,0:T(8,128)(2,1)S(1)} %get-tuple-element.48), channel_id=1, source_target_pairs={{0,4},{1,5},{2,6},{3,7},{4,0},{5,1},{6,2},{7,3},{8,12},{9,13},{10,... | collective-permute-start | bytes 196616 | tf_op jit(solution)/shard_map/ppermute | solution.py:219
  86.3 5.6 %collective-permute-start.21 = (f32[1,128]{1,0:T(1,128)S(1)}, f32[1,128]{1,0:T(1,128)S(1)}, u32[]{:S(2)}, u32[]{:S(2)}) collective-permute-start(f32[1,128]{1,0:T(1,128)S(1)} %broadcast_in_dim.2), channel_id=1, source_target_pairs={{0,16},{8,24},{16,0},{24,8},{1,17},{9,25},{17,1},{25,9},{2,18},{10... | collective-permute-start | bytes 1544 | tf_op jit(solution)/shard_map/ppermute | solution.py:216
  87.7 6.7 %collective-permute-start.22 = (f32[1,128]{1,0:T(1,128)S(1)}, f32[1,128]{1,0:T(1,128)S(1)}, u32[]{:S(2)}, u32[]{:S(2)}) collective-permute-start(f32[1,128]{1,0:T(1,128)S(1)} %broadcast_in_dim.2), channel_id=1, source_target_pairs={{0,24},{8,16},{16,8},{24,0},{1,25},{9,17},{17,9},{25,1},{2,26},{10... | collective-permute-start | bytes 1544 | tf_op jit(solution)/shard_map/ppermute | solution.py:216
  89.1 5.3 %collective-permute-start.20 = (f32[1,128]{1,0:T(1,128)S(1)}, f32[1,128]{1,0:T(1,128)S(1)}, u32[]{:S(2)}, u32[]{:S(2)}) collective-permute-start(f32[1,128]{1,0:T(1,128)S(1)} %broadcast_in_dim.2), channel_id=1, source_target_pairs={{0,8},{8,0},{16,24},{24,16},{1,9},{9,1},{17,25},{25,17},{2,10},{10... | collective-permute-start | bytes 1544 | tf_op jit(solution)/shard_map/ppermute | solution.py:216
  89.9 15.4 %copy-start.7 = (bf16[128,384]{1,0:T(8,128)(2,1)}, bf16[128,384]{1,0:T(8,128)(2,1)S(1)}, u32[]{:S(2)}) copy-start(bf16[128,384]{1,0:T(8,128)(2,1)S(1)} %fusion.2.rest_0_) | copy-start | bytes 294916
  89.9 11.7 %collective-permute-start.29 = (bf16[128,384]{1,0:T(8,128)(2,1)S(1)}, bf16[128,384]{1,0:T(8,128)(2,1)S(1)}, u32[]{:S(2)}, u32[]{:S(2)}) collective-permute-start(bf16[128,384]{1,0:T(8,128)(2,1)S(1)} %fusion.2.rest_0_), channel_id=1, source_target_pairs={{0,6},{1,7},{2,4},{3,5},{4,2},{5,3},{6,0},{7,1},{8,14},{9,15},{10,... | collective-permute-start | bytes 294920 | tf_op jit(solution)/shard_map/ppermute | solution.py:219
  91.9 10.1 %collective-permute-start.28 = (bf16[128,384]{1,0:T(8,128)(2,1)S(1)}, bf16[128,384]{1,0:T(8,128)(2,1)S(1)}, u32[]{:S(2)}, u32[]{:S(2)}) collective-permute-start(bf16[128,384]{1,0:T(8,128)(2,1)S(1)} %fusion.2.rest_0_), channel_id=1, source_target_pairs={{0,4},{1,5},{2,6},{3,7},{4,0},{5,1},{6,2},{7,3},{8,12},{9,13},{10,... | collective-permute-start | bytes 294920 | tf_op jit(solution)/shard_map/ppermute | solution.py:219
  91.9 10.2 %collective-permute-start.27 = (bf16[128,384]{1,0:T(8,128)(2,1)S(1)}, bf16[128,384]{1,0:T(8,128)(2,1)S(1)}, u32[]{:S(2)}, u32[]{:S(2)}) collective-permute-start(bf16[128,384]{1,0:T(8,128)(2,1)S(1)} %fusion.2.rest_0_), channel_id=1, source_target_pairs={{0,2},{1,3},{2,0},{3,1},{4,6},{5,7},{6,4},{7,5},{8,10},{9,11},{10,... | collective-permute-start | bytes 294920 | tf_op jit(solution)/shard_map/ppermute | solution.py:219
  95.0 5.4 %collective-permute-start.25 = (f32[1,128]{1,0:T(1,128)S(1)}, f32[1,128]{1,0:T(1,128)S(1)}, u32[]{:S(2)}, u32[]{:S(2)}) collective-permute-start(f32[1,128]{1,0:T(1,128)S(1)} %add_add_fusion.2), channel_id=1, source_target_pairs={{0,6},{1,7},{2,4},{3,5},{4,2},{5,3},{6,0},{7,1},{8,14},{9,15},{10,... | collective-permute-start | bytes 1544 | tf_op jit(solution)/shard_map/ppermute | solution.py:219
  97.1 4.5 %collective-permute-start.24 = (f32[1,128]{1,0:T(1,128)S(1)}, f32[1,128]{1,0:T(1,128)S(1)}, u32[]{:S(2)}, u32[]{:S(2)}) collective-permute-start(f32[1,128]{1,0:T(1,128)S(1)} %add_add_fusion.2), channel_id=1, source_target_pairs={{0,4},{1,5},{2,6},{3,7},{4,0},{5,1},{6,2},{7,3},{8,12},{9,13},{10,... | collective-permute-start | bytes 1544 | tf_op jit(solution)/shard_map/ppermute | solution.py:219
  100.4 3.6 %collective-permute-start.23 = (f32[1,128]{1,0:T(1,128)S(1)}, f32[1,128]{1,0:T(1,128)S(1)}, u32[]{:S(2)}, u32[]{:S(2)}) collective-permute-start(f32[1,128]{1,0:T(1,128)S(1)} %add_add_fusion.2), channel_id=1, source_target_pairs={{0,2},{1,3},{2,0},{3,1},{4,6},{5,7},{6,4},{7,5},{8,10},{9,11},{10,... | collective-permute-start | bytes 1544 | tf_op jit(solution)/shard_map/ppermute | solution.py:219
  101.5 3.7 %collective-permute-start.30 = (bf16[128,384]{1,0:T(8,128)(2,1)S(1)}, bf16[128,384]{1,0:T(8,128)(2,1)S(1)}, u32[]{:S(2)}, u32[]{:S(2)}) collective-permute-start(bf16[128,384]{1,0:T(8,128)(2,1)S(1)} %fusion.2.rest_0_), channel_id=1, source_target_pairs={{0,1},{1,0},{2,3},{3,2},{4,5},{5,4},{6,7},{7,6},{8,9},{9,8},{10,11... | collective-permute-start | bytes 294920 | tf_op jit(solution)/shard_map/ppermute | solution.py:219
  101.5 3.7 %copy-start.12 = (bf16[128,384]{1,0:T(8,128)(2,1)}, bf16[128,384]{1,0:T(8,128)(2,1)S(1)}, u32[]{:S(2)}) copy-start(bf16[128,384]{1,0:T(8,128)(2,1)S(1)} %collective-permute-done.29.rest_3_) | copy-start | bytes 294916
  101.5 3.6 %collective-permute-start.33 = (bf16[128,384]{1,0:T(8,128)(2,1)S(1)}, bf16[128,384]{1,0:T(8,128)(2,1)S(1)}, u32[]{:S(2)}, u32[]{:S(2)}) collective-permute-start(bf16[128,384]{1,0:T(8,128)(2,1)S(1)} %collective-permute-done.29.rest_3_), channel_id=1, source_target_pairs={{0,1},{1,0},{2,3},{3,2},{4,5},{5,4},{6,7},{7,6},{8,9},{9,8},{10,11... | collective-permute-start | bytes 294920 | tf_op jit(solution)/shard_map/ppermute | solution.py:219
  102.1 3.2 %copy-start.13 = (bf16[128,384]{1,0:T(8,128)(2,1)}, bf16[128,384]{1,0:T(8,128)(2,1)S(1)}, u32[]{:S(2)}) copy-start(bf16[128,384]{1,0:T(8,128)(2,1)S(1)} %collective-permute-done.28.rest_2_) | copy-start | bytes 294916
  102.1 3.2 %collective-permute-start.32 = (bf16[128,384]{1,0:T(8,128)(2,1)S(1)}, bf16[128,384]{1,0:T(8,128)(2,1)S(1)}, u32[]{:S(2)}, u32[]{:S(2)}) collective-permute-start(bf16[128,384]{1,0:T(8,128)(2,1)S(1)} %collective-permute-done.28.rest_2_), channel_id=1, source_target_pairs={{0,1},{1,0},{2,3},{3,2},{4,5},{5,4},{6,7},{7,6},{8,9},{9,8},{10,11... | collective-permute-start | bytes 294920 | tf_op jit(solution)/shard_map/ppermute | solution.py:219
  102.1 3.1 %copy-start.14 = (bf16[128,384]{1,0:T(8,128)(2,1)}, bf16[128,384]{1,0:T(8,128)(2,1)S(1)}, u32[]{:S(2)}) copy-start(bf16[128,384]{1,0:T(8,128)(2,1)S(1)} %collective-permute-done.27.rest_1_) | copy-start | bytes 294916
  102.1 3.1 %collective-permute-start.31 = (bf16[128,384]{1,0:T(8,128)(2,1)S(1)}, bf16[128,384]{1,0:T(8,128)(2,1)S(1)}, u32[]{:S(2)}, u32[]{:S(2)}) collective-permute-start(bf16[128,384]{1,0:T(8,128)(2,1)S(1)} %collective-permute-done.27.rest_1_), channel_id=1, source_target_pairs={{0,1},{1,0},{2,3},{3,2},{4,5},{5,4},{6,7},{7,6},{8,9},{9,8},{10,11... | collective-permute-start | bytes 294920 | tf_op jit(solution)/shard_map/ppermute | solution.py:219
  104.0 1.3 %copy-start.19 = (f32[1,128]{1,0:T(1,128)}, f32[1,128]{1,0:T(1,128)S(1)}, u32[]{:S(2)}) copy-start(f32[1,128]{1,0:T(1,128)S(1)} %add_add_fusion.1.line) | copy-start | bytes 1540
  104.0 1.2 %collective-permute-start.26 = (f32[1,128]{1,0:T(1,128)S(1)}, f32[1,128]{1,0:T(1,128)S(1)}, u32[]{:S(2)}, u32[]{:S(2)}) collective-permute-start(f32[1,128]{1,0:T(1,128)S(1)} %add_add_fusion.1.line), channel_id=1, source_target_pairs={{0,1},{1,0},{2,3},{3,2},{4,5},{5,4},{6,7},{7,6},{8,9},{9,8},{10,11... | collective-permute-start | bytes 1544 | tf_op jit(solution)/shard_map/ppermute | solution.py:219
  (8 other events, 5.3 us)

commit v2 on v1

--- a/solution.py
+++ b/solution.py
@@ -136,15 +136,6 @@
         out[:, shard_cols(index, mask, width)] = total.astype(out.dtype)
 
 
-def pack_kernel(mask, info, keep, arrived, part, out):
-    rows, ohalf = keep.shape[0], part.shape[2]
-    mid = part.shape[1] // 2
-    total = keep[...].astype(jnp.float32) + arrived[...].astype(jnp.float32)
-    out[:rows] = total.astype(out.dtype)
-    out[rows:, :ohalf] = part[mask, :mid].astype(out.dtype)
-    out[rows:, ohalf:] = part[mask, mid:].astype(out.dtype)
-
-
 def finish_kernel(count, half, info, line, away, *rest):
     pieces, out, norm = rest[:-2], rest[-2], rest[-1]
     norm_sq = line[...] + away[...]
@@ -241,19 +232,11 @@
     out_keep, out_send = vmem_call(
         functools.partial(out_terms_kernel, shards), [out_shape] * 2, waits=4
     )(info, out_grad, attn_saved, cosine, sines, allowed, row_lse)
-    theirs = [to_member(chunk, 1) for chunk in mine]
-    piece_rows = width // groups
-
-    def reduce_groups(total, axis):
-        low = total.astype(bf16)
-        piece = lax.dynamic_slice_in_dim(total, place * piece_rows, piece_rows, axis)
-        for mask in range(1, groups):
-            away = lax.dynamic_slice_in_dim(low, (place ^ mask) * piece_rows, piece_rows, axis)
-            piece = piece + to_member(away, 2 * mask).astype(jnp.float32)
-        return piece
-
     out_sum = out_keep.astype(jnp.float32) + to_member(out_send, 1).astype(jnp.float32)
-    out_part = reduce_groups(out_sum, 1)
+    out_low = [out_sum[mask].astype(bf16) for mask in range(1, shards)]
+    out_low, fence = lax.optimization_barrier((out_low, mine))
+    theirs = [to_member(chunk, 1) for chunk in fence]
+    out_got = [to_shard(low, mask + 1) for mask, low in enumerate(out_low)]
 
     qkv_shape = jax.ShapeDtypeStruct((width, half), bf16)
     results = vmem_call(
@@ -264,24 +247,30 @@
             pltpu.VMEM((rows, w_out_t.shape[1]), jnp.float32),
         ],
     )(info, hidden_in, out_grad, attn_saved, row_lse, cosine, sines, allowed, w_qkv, w_out_t,
-      *mine, *theirs)
+      *fence, *theirs)
     d_qkv, keep, send = results[0], results[1 : shards + 1], results[shards + 1 :]
     input_grad = vmem_call(
         functools.partial(input_kernel, shards), jax.ShapeDtypeStruct(hidden_in.shape, bf16)
-    )(info, d_qkv, w_qkv, *mine, *theirs)
-
-    mid = piece_rows // 2
-    got = []
+    )(info, d_qkv, w_qkv, *fence, *theirs)
+
+    qkv_got = []
     for mask in list(range(1, shards)) + [0]:
-        kind = bf16 if mask else jnp.float32
-        both = vmem_call(
-            functools.partial(pack_kernel, mask), jax.ShapeDtypeStruct((width + mid, half), kind)
-        )(info, keep[mask], to_member(send[mask], 1), out_part)
-        got.append(to_shard(both, mask) if mask else both)
-    got, input_grad = lax.optimization_barrier((got, input_grad))
-    total = sum(part.astype(jnp.float32) for part in got)
-    out_piece = jnp.concatenate([total[width:, :ohalf], total[width:, ohalf:]], axis=0)
-    piece = jnp.concatenate([reduce_groups(total[:width], 0), out_piece], axis=1)
+        both = keep[mask].astype(jnp.float32) + to_member(send[mask], 1).astype(jnp.float32)
+        qkv_got.append(to_shard(both.astype(bf16), mask) if mask else both)
+    qkv_got, out_got, input_grad = lax.optimization_barrier((qkv_got, out_got, input_grad))
+    total = jnp.concatenate(
+        [
+            sum(part.astype(jnp.float32) for part in qkv_got),
+            sum((part.astype(jnp.float32) for part in out_got), out_sum[0]),
+        ],
+        axis=1,
+    )
+    low = total.astype(bf16)
+    piece_rows = width // groups
+    piece = lax.dynamic_slice_in_dim(total, place * piece_rows, piece_rows, 0)
+    for mask in range(1, groups):
+        away = lax.dynamic_slice_in_dim(low, (place ^ mask) * piece_rows, piece_rows, 0)
+        piece = piece + to_member(away, 2 * mask).astype(jnp.float32)
     low = piece.astype(bf16)
     square = jnp.full((1, 128), jnp.sum(jnp.square(piece)), jnp.float32)
     own = [low] + [to_member(low, 2 * mask) for mask in range(1, groups)]

time: 109 us -> 106 us (0.972)
  Pallas kernels: 25.1 us -> 17.4 us
  waiting for transfers between devices: 35.6 us -> 42.8 us
  local copies, waits for them, and re-layouts: 9.42 us -> 5.15 us
  starting transfers between devices: 28.1 us -> 29.5 us
    pallas_call x9 -> x5, Pallas kernels: 25.1 us -> 17.4 us  [call(): pl.pallas_call(kernel, out_shape=outs, in_specs=[SMEM] + [VMEM] * (len(ar...]
    ppermute x9 -> x12, waiting for transfers between devices: 19.2 us -> 26.8 us  [to_shard(): return lax.ppermute(value, 'fsdp', [(i, i ^ mask) for i in range(shards)])]
    unnamed x45 -> x39, local copies, waits for them, and re-layouts: 7.9 us -> 3.73 us
    ppermute x9 -> x12, starting transfers between devices: 11 us -> 14.8 us  [to_shard(): return lax.ppermute(value, 'fsdp', [(i, i ^ mask) for i in range(shards)])]
    add x3, other arithmetic: 2.86 us -> 0.22 us  [the longest x1 0.11 us: body(): sum((part.astype(jnp.float32) for part in qkv_got))]
    ppermute x25 -> x22, starting transfers between devices: 17.1 us -> 14.7 us  [to_member(): return lax.ppermute(value, 'rep', [(i, i ^ mask) for i in range(copies)])]
    convert_element_type x0 -> x4, other arithmetic: none -> 2.15 us  [the longest x3 2.1 us: body(): qkv_got.append(to_shard(both.astype(bf16), mask) if mask else both)]
    ppermute x25 -> x22, waiting for transfers between devices: 16.4 us -> 16 us  [to_member(): return lax.ppermute(value, 'rep', [(i, i ^ mask) for i in range(copies)])]
  transfers between devices with their start and end apart: 34 -> 34, of which waited for: 13 -> 12; matrix products, arithmetic and copies ran while one was open for 4% -> 4% of each run, Pallas kernels for 18% -> 5%
where the time goes in v2:
time: 106 us; the launch traced here: 105 us
  waiting for transfers between devices  42.8 us (40%)
  starting transfers between devices  29.5 us (28%)
  Pallas kernels  17.4 us (16%)
  other arithmetic  8.69 us (8%)
  local copies, waits for them, and re-layouts  5.15 us (5%)
  between operations  1.58 us (1%)
    ppermute x12, waiting for transfers between devices, to_shard(): return lax.ppermute(value, 'fsdp', [(i, i ^ mask) for i in range(shards)])  26.8 us
    pallas_call x5, Pallas kernels, call(): pl.pallas_call(kernel, out_shape=outs, in_specs=[SMEM] + [VMEM] * (len(ar...  17.4 us
    ppermute x22, waiting for transfers between devices, to_member(): return lax.ppermute(value, 'rep', [(i, i ^ mask) for i in range(copies)])  16 us
    ppermute x12, starting transfers between devices, to_shard(): return lax.ppermute(value, 'fsdp', [(i, i ^ mask) for i in range(shards)])  14.8 us
    ppermute x22, starting transfers between devices, to_member(): return lax.ppermute(value, 'rep', [(i, i ^ mask) for i in range(copies)])  14.7 us
    unnamed x39, local copies, waits for them, and re-layouts  3.73 us
  transfers between devices with their start and end apart: 34, of which 12 were waited for; matrix products, arithmetic and copies ran while one was open for 4% of the time, Pallas kernels for 5%

profile of v2, /device:TPU:0, one launch (start us, length us, event | category | flops | bytes accessed | tf_op | source)
XLA Modules:
  0.0 105.2 jit_solution(5172755480995459023)
XLA Ops:
  0.7 1.5 %copy.14.rest_3_.lse = f32[256,2]{1,0:T(8,128)} copy(f32[256,2]{0,1:T(2,128)} %param.11) | data formatting | bytes 4096 | tf_op args[3]
  2.8 0.8 reduce-window.8
  3.7 0.8 fusion.5.rest_2_.allowed
  4.5 0.5 fusion.10
  5.1 0.7 pad_add_fusion.info
  5.8 0.8 pad_maximum_fusion.1
  6.6 3.0 %shard_map.103 = (bf16[4,512,128]{2,1,0:T(8,128)(2,1)}, bf16[4,512,128]{2,1,0:T(8,128)(2,1)}) custom-call(s32[3]{0:T(128)} %pad_add_fusion.info, bf16[256,2048]{1,0:T(8,128)(2,1)} %out_grad.3, bf16[256,256]{1,0:T(8,128)(2,1)} %saved.3, f32[256,128]{1,0:T(8,128)} %get-tuple-element.70.rest_0_.cosine, f32[256,128]{1,0:T(8,128)} %get-tuple-element.71.rest_1_.sines, ...), custom_call_target="tpu_custom_call" | custom-call | tf_op jit(solution)/shard_map/pallas_call | solution.py:163
  10.0 1.9 %shard_map.104 = bf16[512,384]{1,0:T(8,128)(2,1)} custom-call(s32[3]{0:T(128)} %pad_add_fusion.info, bf16[512,512]{1,0:T(8,128)(2,1)} %w_qkv.5, bf16[512,256]{1,0:T(8,128)(2,1)} %w_out.3), custom_call_target="tpu_custom_call" | custom-call | tf_op jit(solution)/shard_map/pallas_call | solution.py:163
  12.0 2.5 %collective-permute-start.1 = (bf16[512,384]{1,0:T(8,128)(2,1)}, bf16[512,384]{1,0:T(8,128)(2,1)S(1)}, u32[]{:S(2)}, u32[]{:S(2)}) collective-permute-start(bf16[512,384]{1,0:T(8,128)(2,1)} %shard_map.104), channel_id=1, source_target_pairs={{0,8},{8,0},{16,24},{24,16},{1,9},{9,1},{17,25},{25,17},{2,10},{10... | collective-permute-start | bytes 1179656 | tf_op jit(solution)/shard_map/ppermute | solution.py:207
  14.5 1.5 %collective-permute-start.2 = (bf16[512,384]{1,0:T(8,128)(2,1)}, bf16[512,384]{1,0:T(8,128)(2,1)S(1)}, u32[]{:S(2)}, u32[]{:S(2)}) collective-permute-start(bf16[512,384]{1,0:T(8,128)(2,1)} %shard_map.104), channel_id=1, source_target_pairs={{0,16},{8,24},{16,0},{24,8},{1,17},{9,25},{17,1},{25,9},{2,18},{10... | collective-permute-start | bytes 1179656 | tf_op jit(solution)/shard_map/ppermute | solution.py:207
  16.0 1.2 %convert_add_fusion = (f32[4,512,128]{2,1,0:T(8,128)S(1)}, bf16[4,512,128]{2,1,0:T(8,128)(2,1)S(1)}) fusion(bf16[4,512,128]{2,1,0:T(8,128)(2,1)S(1)} %collective-permute-done, bf16[4,512,128]{2,1,0:T(8,128)(2,1)} %get-tuple-element.30), kind=kLoop, calls=%fused_computation | loop fusion | flops 1048576 | bytes 2621440 | tf_op jit(solution)/shard_map/add | solution.py:235
  17.2 0.7 slice_bitcast_fusion.1
  17.9 6.7 %collective-permute-done.1.rest_0_ = bf16[512,384]{1,0:T(8,128)(2,1)S(1)} collective-permute-done((bf16[512,384]{1,0:T(8,128)(2,1)}, bf16[512,384]{1,0:T(8,128)(2,1)S(1)}, u32[]{:S(2)}, u32[]{:S(2)}) %collective-permute-start.1) | collective-permute-done | bytes 393248 | tf_op jit(solution)/shard_map/ppermute | solution.py:207
  24.6 9.7 %collective-permute-done.2.rest_1_ = bf16[512,384]{1,0:T(8,128)(2,1)S(1)} collective-permute-done((bf16[512,384]{1,0:T(8,128)(2,1)}, bf16[512,384]{1,0:T(8,128)(2,1)S(1)}, u32[]{:S(2)}, u32[]{:S(2)}) %collective-permute-start.2) | collective-permute-done | bytes 393248 | tf_op jit(solution)/shard_map/ppermute | solution.py:207
  35.0 1.1 %collective-permute-done.4.rest_3_ = bf16[512,384]{1,0:T(8,128)(2,1)S(1)} collective-permute-done((bf16[512,384]{1,0:T(8,128)(2,1)S(1)}, bf16[512,384]{1,0:T(8,128)(2,1)S(1)}, u32[]{:S(2)}, u32[]{:S(2)}) %collective-permute-start.4) | collective-permute-done | bytes 393248 | tf_op jit(solution)/shard_map/ppermute | solution.py:210
  36.1 0.6 collective-permute-done.5.rest_4_
  36.7 0.6 collective-permute-done.6.rest_5_
  37.5 0.7 copy-done.5
  38.2 6.5 %shard_map.105 = (bf16[256,512]{1,0:T(8,128)(2,1)}, bf16[512,256]{1,0:T(8,128)(2,1)}, bf16[512,256]{1,0:T(8,128)(2,1)}, bf16[512,256]{1,0:T(8,128)(2,1)}, bf16[5...) custom-call(s32[3]{0:T(128)} %pad_add_fusion.info, ...), custom_call_target="tpu_custom_call" | custom-call | tf_op jit(solution)/shard_map/pallas_call | solution.py:163
  45.3 1.2 %collective-permute-start.14 = (bf16[512,128]{1,0:T(8,128)(2,1)}, bf16[512,128]{1,0:T(8,128)(2,1)S(1)}, u32[]{:S(2)}, u32[]{:S(2)}) collective-permute-start(bf16[512,128]{1,0:T(8,128)(2,1)} %get-tuple-element.43), channel_id=1, source_target_pairs={{0,8},{8,0},{16,24},{24,16},{1,9},{9,1},{17,25},{25,17},{2,10},{10... | collective-permute-start | bytes 393224 | tf_op jit(solution)/shard_map/ppermute | solution.py:207
  46.9 1.0 add_convert_fusion.2
  48.0 0.9 collective-permute-start.8
  48.9 1.0 add_convert_fusion.1
  49.9 1.6 %collective-permute-start.10 = (bf16[512,256]{1,0:T(8,128)(2,1)S(1)}, bf16[512,256]{1,0:T(8,128)(2,1)S(1)}, u32[]{:S(2)}, u32[]{:S(2)}) collective-permute-start(bf16[512,256]{1,0:T(8,128)(2,1)S(1)} %add_convert_fusion.1), channel_id=1, source_target_pairs={{0,16},{8,24},{16,0},{24,8},{1,17},{9,25},{17,1},{25,9},{2,18},{10... | collective-permute-start | bytes 786440 | tf_op jit(solution)/shard_map/ppermute | solution.py:207
  51.6 1.2 %collective-permute-start.12 = (bf16[512,256]{1,0:T(8,128)(2,1)S(1)}, bf16[512,256]{1,0:T(8,128)(2,1)S(1)}, u32[]{:S(2)}, u32[]{:S(2)}) collective-permute-start(bf16[512,256]{1,0:T(8,128)(2,1)S(1)} %add_convert_fusion), channel_id=1, source_target_pairs={{0,24},{8,16},{16,8},{24,0},{1,25},{9,17},{17,9},{25,1},{2,26},{10... | collective-permute-start | bytes 786440 | tf_op jit(solution)/shard_map/ppermute | solution.py:207
  52.8 3.6 %shard_map.106 = bf16[256,2048]{1,0:T(8,128)(2,1)} custom-call(s32[3]{0:T(128)} %pad_add_fusion.info, bf16[256,512]{1,0:T(8,128)(2,1)} %get-tuple-element.46.d_qkv, bf16[512,512]{1,0:T(8,128)(2,1)} %w_qkv.5, bf16[512,384]{1,0:T(8,128)(2,1)} %copy-done, bf16[512,384]{1,0:T(8,128)(2,1)} %copy-done.1, bf16[512,384]{1,0:T(8,128)(2,1)} %copy-done.2, ...), custom_call_target="tpu_custom_call" | custom-call | tf_op jit(solution)/shard_map/pallas_call | solution.py:163
  56.4 1.1 %collective-permute-start.15 = (bf16[512,128]{1,0:T(8,128)(2,1)S(1)}, bf16[512,128]{1,0:T(8,128)(2,1)S(1)}, u32[]{:S(2)}, u32[]{:S(2)}) collective-permute-start(bf16[512,128]{1,0:T(8,128)(2,1)S(1)} %copy-done.9), channel_id=1, source_target_pairs={{0,16},{8,24},{16,0},{24,8},{1,17},{9,25},{17,1},{25,9},{2,18},{10... | collective-permute-start | bytes 393224 | tf_op jit(solution)/shard_map/ppermute | solution.py:207
  57.5 1.3 %collective-permute-start.16 = (bf16[512,128]{1,0:T(8,128)(2,1)S(1)}, bf16[512,128]{1,0:T(8,128)(2,1)S(1)}, u32[]{:S(2)}, u32[]{:S(2)}) collective-permute-start(bf16[512,128]{1,0:T(8,128)(2,1)S(1)} %get-tuple-element.45), channel_id=1, source_target_pairs={{0,24},{8,16},{16,8},{24,0},{1,25},{9,17},{17,9},{25,1},{2,26},{10... | collective-permute-start | bytes 393224 | tf_op jit(solution)/shard_map/ppermute | solution.py:207
  58.8 10.3 %collective-permute-done.15 = bf16[512,128]{1,0:T(8,128)(2,1)S(1)} collective-permute-done((bf16[512,128]{1,0:T(8,128)(2,1)S(1)}, bf16[512,128]{1,0:T(8,128)(2,1)S(1)}, u32[]{:S(2)}, u32[]{:S(2)}) %collective-permute-start.15) | collective-permute-done | bytes 131104 | tf_op jit(solution)/shard_map/ppermute | solution.py:207
  69.5 3.7 %collective-permute-start.19 = (bf16[128,384]{1,0:T(8,128)(2,1)S(1)}, bf16[128,384]{1,0:T(8,128)(2,1)S(1)}, u32[]{:S(2)}, u32[]{:S(2)}) collective-permute-start(bf16[128,384]{1,0:T(8,128)(2,1)S(1)} %get-tuple-element.65), channel_id=1, source_target_pairs={{0,6},{1,7},{2,4},{3,5},{4,2},{5,3},{6,0},{7,1},{8,14},{9,15},{10,... | collective-permute-start | bytes 294920 | tf_op jit(solution)/shard_map/ppermute | solution.py:210
  73.1 0.8 collective-permute-start.17
  73.9 2.9 %collective-permute-done.19 = bf16[128,384]{1,0:T(8,128)(2,1)S(1)} collective-permute-done((bf16[128,384]{1,0:T(8,128)(2,1)S(1)}, bf16[128,384]{1,0:T(8,128)(2,1)S(1)}, u32[]{:S(2)}, u32[]{:S(2)}) %collective-permute-start.19) | collective-permute-done | bytes 98336 | tf_op jit(solution)/shard_map/ppermute | solution.py:210
  76.8 4.5 %collective-permute-done.18 = bf16[128,384]{1,0:T(8,128)(2,1)S(1)} collective-permute-done((bf16[128,384]{1,0:T(8,128)(2,1)S(1)}, bf16[128,384]{1,0:T(8,128)(2,1)S(1)}, u32[]{:S(2)}, u32[]{:S(2)}) %collective-permute-start.18) | collective-permute-done | bytes 98336 | tf_op jit(solution)/shard_map/ppermute | solution.py:210
  81.4 0.6 multiply_reduce_fusion
  82.0 0.6 broadcast_in_dim.2
  82.7 0.7 collective-permute-start.21
  83.4 1.4 %collective-permute-start.22 = (f32[1,128]{1,0:T(1,128)S(1)}, f32[1,128]{1,0:T(1,128)S(1)}, u32[]{:S(2)}, u32[]{:S(2)}) collective-permute-start(f32[1,128]{1,0:T(1,128)S(1)} %broadcast_in_dim.2), channel_id=1, source_target_pairs={{0,24},{8,16},{16,8},{24,0},{1,25},{9,17},{17,9},{25,1},{2,26},{10... | collective-permute-start | bytes 1544 | tf_op jit(solution)/shard_map/ppermute | solution.py:207
  84.8 1.4 %collective-permute-start.20 = (f32[1,128]{1,0:T(1,128)S(1)}, f32[1,128]{1,0:T(1,128)S(1)}, u32[]{:S(2)}, u32[]{:S(2)}) collective-permute-start(f32[1,128]{1,0:T(1,128)S(1)} %broadcast_in_dim.2), channel_id=1, source_target_pairs={{0,8},{8,0},{16,24},{24,16},{1,9},{9,1},{17,25},{25,17},{2,10},{10... | collective-permute-start | bytes 1544 | tf_op jit(solution)/shard_map/ppermute | solution.py:207
  86.2 0.5 collective-permute-start.27
  86.7 2.6 %collective-permute-start.28 = (bf16[128,384]{1,0:T(8,128)(2,1)S(1)}, bf16[128,384]{1,0:T(8,128)(2,1)S(1)}, u32[]{:S(2)}, u32[]{:S(2)}) collective-permute-start(bf16[128,384]{1,0:T(8,128)(2,1)S(1)} %get-tuple-element.57.rest_0_), channel_id=1, source_target_pairs={{0,4},{1,5},{2,6},{3,7},{4,0},{5,1},{6,2},{7,3},{8,12},{9,13},{10,... | collective-permute-start | bytes 294920 | tf_op jit(solution)/shard_map/ppermute | solution.py:210
  89.3 1.3 %collective-permute-start.29 = (bf16[128,384]{1,0:T(8,128)(2,1)S(1)}, bf16[128,384]{1,0:T(8,128)(2,1)S(1)}, u32[]{:S(2)}, u32[]{:S(2)}) collective-permute-start(bf16[128,384]{1,0:T(8,128)(2,1)S(1)} %get-tuple-element.57.rest_0_), channel_id=1, source_target_pairs={{0,6},{1,7},{2,4},{3,5},{4,2},{5,3},{6,0},{7,1},{8,14},{9,15},{10,... | collective-permute-start | bytes 294920 | tf_op jit(solution)/shard_map/ppermute | solution.py:210
  90.6 0.7 add_add_fusion.2
  91.5 2.4 %collective-permute-start.25 = (f32[1,128]{1,0:T(1,128)S(1)}, f32[1,128]{1,0:T(1,128)S(1)}, u32[]{:S(2)}, u32[]{:S(2)}) collective-permute-start(f32[1,128]{1,0:T(1,128)S(1)} %add_add_fusion.2), channel_id=1, source_target_pairs={{0,6},{1,7},{2,4},{3,5},{4,2},{5,3},{6,0},{7,1},{8,14},{9,15},{10,... | collective-permute-start | bytes 1544 | tf_op jit(solution)/shard_map/ppermute | solution.py:210
  93.9 2.6 %collective-permute-done.24 = f32[1,128]{1,0:T(1,128)S(1)} collective-permute-done((f32[1,128]{1,0:T(1,128)S(1)}, f32[1,128]{1,0:T(1,128)S(1)}, u32[]{:S(2)}, u32[]{:S(2)}) %collective-permute-start.24) | collective-permute-done | bytes 544 | tf_op jit(solution)/shard_map/ppermute | solution.py:210
  97.9 2.2 %collective-permute-done.23 = f32[1,128]{1,0:T(1,128)S(1)} collective-permute-done((f32[1,128]{1,0:T(1,128)S(1)}, f32[1,128]{1,0:T(1,128)S(1)}, u32[]{:S(2)}, u32[]{:S(2)}) %collective-permute-start.23) | collective-permute-done | bytes 544 | tf_op jit(solution)/shard_map/ppermute | solution.py:210
  100.2 1.2 %collective-permute-done.26.away = f32[1,128]{1,0:T(1,128)S(1)} collective-permute-done((f32[1,128]{1,0:T(1,128)S(1)}, f32[1,128]{1,0:T(1,128)S(1)}, u32[]{:S(2)}, u32[]{:S(2)}) %collective-permute-start.26) | collective-permute-done | bytes 544 | tf_op jit(solution)/shard_map/ppermute | solution.py:210
  102.0 0.6 copy-done.16
  102.7 2.5 %shard_map.107 = (f32[512,768]{1,0:T(8,128)}, f32[1,128]{1,0:T(1,128)}) custom-call(s32[3]{0:T(128)} %pad_add_fusion.info, f32[1,128]{1,0:T(1,128)} %copy-done.17, f32[1,128]{1,0:T(1,128)} %copy-done.18, bf16[128,384]{1,0:T(8,128)(2,1)} %copy-done.6, bf16[128,384]{1,0:T(8,128)(2,1)} %copy-done.10, bf16[128,384]{1,0:T(8,128)(2,1)} %copy-done.11, ...), custom_call_target="tpu_custom_call" | custom-call | tf_op jit(solution)/shard_map/pallas_call | solution.py:163
  (87 shorter events, 5.3 us)
Async XLA Ops:
  9.6 6.4 %collective-permute-start = (bf16[4,512,128]{2,1,0:T(8,128)(2,1)}, bf16[4,512,128]{2,1,0:T(8,128)(2,1)S(1)}, u32[]{:S(2)}, u32[]{:S(2)}) collective-permute-start(bf16[4,512,128]{2,1,0:T(8,128)(2,1)} %get-tuple-element.31), channel_id=1, source_target_pairs={{0,1},{1,0},{2,3},{3,2},{4,5},{5,4},{6,7},{7,6},{8,9},{9,8},{10,11... | collective-permute-start | bytes 1572872 | tf_op jit(solution)/shard_map/ppermute | solution.py:210
  12.0 12.7 %collective-permute-start.1 = (bf16[512,384]{1,0:T(8,128)(2,1)}, bf16[512,384]{1,0:T(8,128)(2,1)S(1)}, u32[]{:S(2)}, u32[]{:S(2)}) collective-permute-start(bf16[512,384]{1,0:T(8,128)(2,1)} %shard_map.104), channel_id=1, source_target_pairs={{0,8},{8,0},{16,24},{24,16},{1,9},{9,1},{17,25},{25,17},{2,10},{10... | collective-permute-start | bytes 1179656 | tf_op jit(solution)/shard_map/ppermute | solution.py:207
  14.5 19.9 %collective-permute-start.2 = (bf16[512,384]{1,0:T(8,128)(2,1)}, bf16[512,384]{1,0:T(8,128)(2,1)S(1)}, u32[]{:S(2)}, u32[]{:S(2)}) collective-permute-start(bf16[512,384]{1,0:T(8,128)(2,1)} %shard_map.104), channel_id=1, source_target_pairs={{0,16},{8,24},{16,0},{24,8},{1,17},{9,25},{17,1},{25,9},{2,18},{10... | collective-permute-start | bytes 1179656 | tf_op jit(solution)/shard_map/ppermute | solution.py:207
  16.0 18.4 %collective-permute-start.3 = (bf16[512,384]{1,0:T(8,128)(2,1)}, bf16[512,384]{1,0:T(8,128)(2,1)S(1)}, u32[]{:S(2)}, u32[]{:S(2)}) collective-permute-start(bf16[512,384]{1,0:T(8,128)(2,1)} %shard_map.104), channel_id=1, source_target_pairs={{0,24},{8,16},{16,8},{24,0},{1,25},{9,17},{17,9},{25,1},{2,26},{10... | collective-permute-start | bytes 1179656 | tf_op jit(solution)/shard_map/ppermute | solution.py:207
  24.6 12.6 %copy-start = (bf16[512,384]{1,0:T(8,128)(2,1)}, bf16[512,384]{1,0:T(8,128)(2,1)S(1)}, u32[]{:S(2)}) copy-start(bf16[512,384]{1,0:T(8,128)(2,1)S(1)} %collective-permute-done.1.rest_0_) | copy-start | bytes 1179652
  34.3 2.9 %copy-start.1 = (bf16[512,384]{1,0:T(8,128)(2,1)}, bf16[512,384]{1,0:T(8,128)(2,1)S(1)}, u32[]{:S(2)}) copy-start(bf16[512,384]{1,0:T(8,128)(2,1)S(1)} %collective-permute-done.2.rest_1_) | copy-start | bytes 1179652
  34.3 2.9 %copy-start.2 = (bf16[512,384]{1,0:T(8,128)(2,1)}, bf16[512,384]{1,0:T(8,128)(2,1)S(1)}, u32[]{:S(2)}) copy-start(bf16[512,384]{1,0:T(8,128)(2,1)S(1)} %collective-permute-done.3.rest_2_) | copy-start | bytes 1179652
  34.3 1.8 %collective-permute-start.4 = (bf16[512,384]{1,0:T(8,128)(2,1)S(1)}, bf16[512,384]{1,0:T(8,128)(2,1)S(1)}, u32[]{:S(2)}, u32[]{:S(2)}) collective-permute-start(bf16[512,384]{1,0:T(8,128)(2,1)S(1)} %collective-permute-done.1.rest_0_), channel_id=1, source_target_pairs={{0,1},{1,0},{2,3},{3,2},{4,5},{5,4},{6,7},{7,6},{8,9},{9,8},{10,11... | collective-permute-start | bytes 1179656 | tf_op jit(solution)/shard_map/ppermute | solution.py:210
  34.4 2.3 %collective-permute-start.5 = (bf16[512,384]{1,0:T(8,128)(2,1)S(1)}, bf16[512,384]{1,0:T(8,128)(2,1)S(1)}, u32[]{:S(2)}, u32[]{:S(2)}) collective-permute-start(bf16[512,384]{1,0:T(8,128)(2,1)S(1)} %collective-permute-done.2.rest_1_), channel_id=1, source_target_pairs={{0,1},{1,0},{2,3},{3,2},{4,5},{5,4},{6,7},{7,6},{8,9},{9,8},{10,11... | collective-permute-start | bytes 1179656 | tf_op jit(solution)/shard_map/ppermute | solution.py:210
  34.9 2.3 %collective-permute-start.6 = (bf16[512,384]{1,0:T(8,128)(2,1)S(1)}, bf16[512,384]{1,0:T(8,128)(2,1)S(1)}, u32[]{:S(2)}, u32[]{:S(2)}) collective-permute-start(bf16[512,384]{1,0:T(8,128)(2,1)S(1)} %collective-permute-done.3.rest_2_), channel_id=1, source_target_pairs={{0,1},{1,0},{2,3},{3,2},{4,5},{5,4},{6,7},{7,6},{8,9},{9,8},{10,11... | collective-permute-start | bytes 1179656 | tf_op jit(solution)/shard_map/ppermute | solution.py:210
  36.1 1.1 %copy-start.3 = (bf16[512,384]{1,0:T(8,128)(2,1)}, bf16[512,384]{1,0:T(8,128)(2,1)S(1)}, u32[]{:S(2)}) copy-start(bf16[512,384]{1,0:T(8,128)(2,1)S(1)} %collective-permute-done.4.rest_3_) | copy-start | bytes 1179652
  36.7 0.8 copy-start.4
  37.5 0.7 copy-start.5
  44.7 6.8 %copy-start.7 = (bf16[512,256]{1,0:T(8,128)(2,1)S(1)}, bf16[512,256]{1,0:T(8,128)(2,1)}, u32[]{:S(2)}) copy-start(bf16[512,256]{1,0:T(8,128)(2,1)} %get-tuple-element.39) | copy-start | bytes 786436
  44.7 2.3 %collective-permute-start.7 = (bf16[512,256]{1,0:T(8,128)(2,1)}, bf16[512,256]{1,0:T(8,128)(2,1)S(1)}, u32[]{:S(2)}, u32[]{:S(2)}) collective-permute-start(bf16[512,256]{1,0:T(8,128)(2,1)} %get-tuple-element.36), channel_id=1, source_target_pairs={{0,1},{1,0},{2,3},{3,2},{4,5},{5,4},{6,7},{7,6},{8,9},{9,8},{10,11... | collective-permute-start | bytes 786440 | tf_op jit(solution)/shard_map/ppermute | solution.py:210
  44.9 4.0 %collective-permute-start.9 = (bf16[512,256]{1,0:T(8,128)(2,1)}, bf16[512,256]{1,0:T(8,128)(2,1)S(1)}, u32[]{:S(2)}, u32[]{:S(2)}) collective-permute-start(bf16[512,256]{1,0:T(8,128)(2,1)} %get-tuple-element.38), channel_id=1, source_target_pairs={{0,1},{1,0},{2,3},{3,2},{4,5},{5,4},{6,7},{7,6},{8,9},{9,8},{10,11... | collective-permute-start | bytes 786440 | tf_op jit(solution)/shard_map/ppermute | solution.py:210
  45.3 11.1 %collective-permute-start.14 = (bf16[512,128]{1,0:T(8,128)(2,1)}, bf16[512,128]{1,0:T(8,128)(2,1)S(1)}, u32[]{:S(2)}, u32[]{:S(2)}) collective-permute-start(bf16[512,128]{1,0:T(8,128)(2,1)} %get-tuple-element.43), channel_id=1, source_target_pairs={{0,8},{8,0},{16,24},{24,16},{1,9},{9,1},{17,25},{25,17},{2,10},{10... | collective-permute-start | bytes 393224 | tf_op jit(solution)/shard_map/ppermute | solution.py:207
  46.4 5.1 %collective-permute-start.11 = (bf16[512,256]{1,0:T(8,128)(2,1)}, bf16[512,256]{1,0:T(8,128)(2,1)S(1)}, u32[]{:S(2)}, u32[]{:S(2)}) collective-permute-start(bf16[512,256]{1,0:T(8,128)(2,1)} %get-tuple-element.40), channel_id=1, source_target_pairs={{0,1},{1,0},{2,3},{3,2},{4,5},{5,4},{6,7},{7,6},{8,9},{9,8},{10,11... | collective-permute-start | bytes 786440 | tf_op jit(solution)/shard_map/ppermute | solution.py:210
  46.4 11.1 %collective-permute-start.13 = (bf16[512,256]{1,0:T(8,128)(2,1)}, bf16[512,256]{1,0:T(8,128)(2,1)S(1)}, u32[]{:S(2)}, u32[]{:S(2)}) collective-permute-start(bf16[512,256]{1,0:T(8,128)(2,1)} %get-tuple-element.42), channel_id=1, source_target_pairs={{0,1},{1,0},{2,3},{3,2},{4,5},{5,4},{6,7},{7,6},{8,9},{9,8},{10,11... | collective-permute-start | bytes 786440 | tf_op jit(solution)/shard_map/ppermute | solution.py:210
  48.0 21.2 %collective-permute-start.8 = (bf16[512,256]{1,0:T(8,128)(2,1)S(1)}, bf16[512,256]{1,0:T(8,128)(2,1)S(1)}, u32[]{:S(2)}, u32[]{:S(2)}) collective-permute-start(bf16[512,256]{1,0:T(8,128)(2,1)S(1)} %add_convert_fusion.2), channel_id=1, source_target_pairs={{0,8},{8,0},{16,24},{24,16},{1,9},{9,1},{17,25},{25,17},{2,10},{10... | collective-permute-start | bytes 786440 | tf_op jit(solution)/shard_map/ppermute | solution.py:207
  49.9 19.2 %collective-permute-start.10 = (bf16[512,256]{1,0:T(8,128)(2,1)S(1)}, bf16[512,256]{1,0:T(8,128)(2,1)S(1)}, u32[]{:S(2)}, u32[]{:S(2)}) collective-permute-start(bf16[512,256]{1,0:T(8,128)(2,1)S(1)} %add_convert_fusion.1), channel_id=1, source_target_pairs={{0,16},{8,24},{16,0},{24,8},{1,17},{9,25},{17,1},{25,9},{2,18},{10... | collective-permute-start | bytes 786440 | tf_op jit(solution)/shard_map/ppermute | solution.py:207
  51.6 17.6 %collective-permute-start.12 = (bf16[512,256]{1,0:T(8,128)(2,1)S(1)}, bf16[512,256]{1,0:T(8,128)(2,1)S(1)}, u32[]{:S(2)}, u32[]{:S(2)}) collective-permute-start(bf16[512,256]{1,0:T(8,128)(2,1)S(1)} %add_convert_fusion), channel_id=1, source_target_pairs={{0,24},{8,16},{16,8},{24,0},{1,25},{9,17},{17,9},{25,1},{2,26},{10... | collective-permute-start | bytes 786440 | tf_op jit(solution)/shard_map/ppermute | solution.py:207
  52.8 3.6 %copy-start.9 = (bf16[512,128]{1,0:T(8,128)(2,1)S(1)}, bf16[512,128]{1,0:T(8,128)(2,1)}, u32[]{:S(2)}) copy-start(bf16[512,128]{1,0:T(8,128)(2,1)} %get-tuple-element.44) | copy-start | bytes 393220
  52.8 6.0 %copy-start.8 = (bf16[512,256]{1,0:T(8,128)(2,1)S(1)}, bf16[512,256]{1,0:T(8,128)(2,1)}, u32[]{:S(2)}) copy-start(bf16[512,256]{1,0:T(8,128)(2,1)} %get-tuple-element.41) | copy-start | bytes 786436
  56.4 12.8 %collective-permute-start.15 = (bf16[512,128]{1,0:T(8,128)(2,1)S(1)}, bf16[512,128]{1,0:T(8,128)(2,1)S(1)}, u32[]{:S(2)}, u32[]{:S(2)}) collective-permute-start(bf16[512,128]{1,0:T(8,128)(2,1)S(1)} %copy-done.9), channel_id=1, source_target_pairs={{0,16},{8,24},{16,0},{24,8},{1,17},{9,25},{17,1},{25,9},{2,18},{10... | collective-permute-start | bytes 393224 | tf_op jit(solution)/shard_map/ppermute | solution.py:207
  57.5 11.6 %collective-permute-start.16 = (bf16[512,128]{1,0:T(8,128)(2,1)S(1)}, bf16[512,128]{1,0:T(8,128)(2,1)S(1)}, u32[]{:S(2)}, u32[]{:S(2)}) collective-permute-start(bf16[512,128]{1,0:T(8,128)(2,1)S(1)} %get-tuple-element.45), channel_id=1, source_target_pairs={{0,24},{8,16},{16,8},{24,0},{1,25},{9,17},{17,9},{25,1},{2,26},{10... | collective-permute-start | bytes 393224 | tf_op jit(solution)/shard_map/ppermute | solution.py:207
  69.5 7.3 %collective-permute-start.19 = (bf16[128,384]{1,0:T(8,128)(2,1)S(1)}, bf16[128,384]{1,0:T(8,128)(2,1)S(1)}, u32[]{:S(2)}, u32[]{:S(2)}) collective-permute-start(bf16[128,384]{1,0:T(8,128)(2,1)S(1)} %get-tuple-element.65), channel_id=1, source_target_pairs={{0,6},{1,7},{2,4},{3,5},{4,2},{5,3},{6,0},{7,1},{8,14},{9,15},{10,... | collective-permute-start | bytes 294920 | tf_op jit(solution)/shard_map/ppermute | solution.py:210
  73.1 8.2 %collective-permute-start.18 = (bf16[128,384]{1,0:T(8,128)(2,1)S(1)}, bf16[128,384]{1,0:T(8,128)(2,1)S(1)}, u32[]{:S(2)}, u32[]{:S(2)}) collective-permute-start(bf16[128,384]{1,0:T(8,128)(2,1)S(1)} %get-tuple-element.66), channel_id=1, source_target_pairs={{0,4},{1,5},{2,6},{3,7},{4,0},{5,1},{6,2},{7,3},{8,12},{9,13},{10,... | collective-permute-start | bytes 294920 | tf_op jit(solution)/shard_map/ppermute | solution.py:210
  73.1 8.2 %collective-permute-start.17 = (bf16[128,384]{1,0:T(8,128)(2,1)S(1)}, bf16[128,384]{1,0:T(8,128)(2,1)S(1)}, u32[]{:S(2)}, u32[]{:S(2)}) collective-permute-start(bf16[128,384]{1,0:T(8,128)(2,1)S(1)} %get-tuple-element.64), channel_id=1, source_target_pairs={{0,2},{1,3},{2,0},{3,1},{4,6},{5,7},{6,4},{7,5},{8,10},{9,11},{10,... | collective-permute-start | bytes 294920 | tf_op jit(solution)/shard_map/ppermute | solution.py:210
  81.4 20.0 %copy-start.6 = (bf16[128,384]{1,0:T(8,128)(2,1)}, bf16[128,384]{1,0:T(8,128)(2,1)S(1)}, u32[]{:S(2)}) copy-start(bf16[128,384]{1,0:T(8,128)(2,1)S(1)} %get-tuple-element.57.rest_0_) | copy-start | bytes 294916
  82.7 6.6 %collective-permute-start.21 = (f32[1,128]{1,0:T(1,128)S(1)}, f32[1,128]{1,0:T(1,128)S(1)}, u32[]{:S(2)}, u32[]{:S(2)}) collective-permute-start(f32[1,128]{1,0:T(1,128)S(1)} %broadcast_in_dim.2), channel_id=1, source_target_pairs={{0,16},{8,24},{16,0},{24,8},{1,17},{9,25},{17,1},{25,9},{2,18},{10... | collective-permute-start | bytes 1544 | tf_op jit(solution)/shard_map/ppermute | solution.py:207
  83.4 7.2 %collective-permute-start.22 = (f32[1,128]{1,0:T(1,128)S(1)}, f32[1,128]{1,0:T(1,128)S(1)}, u32[]{:S(2)}, u32[]{:S(2)}) collective-permute-start(f32[1,128]{1,0:T(1,128)S(1)} %broadcast_in_dim.2), channel_id=1, source_target_pairs={{0,24},{8,16},{16,8},{24,0},{1,25},{9,17},{17,9},{25,1},{2,26},{10... | collective-permute-start | bytes 1544 | tf_op jit(solution)/shard_map/ppermute | solution.py:207
  84.8 5.8 %collective-permute-start.20 = (f32[1,128]{1,0:T(1,128)S(1)}, f32[1,128]{1,0:T(1,128)S(1)}, u32[]{:S(2)}, u32[]{:S(2)}) collective-permute-start(f32[1,128]{1,0:T(1,128)S(1)} %broadcast_in_dim.2), channel_id=1, source_target_pairs={{0,8},{8,0},{16,24},{24,16},{1,9},{9,1},{17,25},{25,17},{2,10},{10... | collective-permute-start | bytes 1544 | tf_op jit(solution)/shard_map/ppermute | solution.py:207
  86.2 10.6 %collective-permute-start.27 = (bf16[128,384]{1,0:T(8,128)(2,1)S(1)}, bf16[128,384]{1,0:T(8,128)(2,1)S(1)}, u32[]{:S(2)}, u32[]{:S(2)}) collective-permute-start(bf16[128,384]{1,0:T(8,128)(2,1)S(1)} %get-tuple-element.57.rest_0_), channel_id=1, source_target_pairs={{0,2},{1,3},{2,0},{3,1},{4,6},{5,7},{6,4},{7,5},{8,10},{9,11},{10,... | collective-permute-start | bytes 294920 | tf_op jit(solution)/shard_map/ppermute | solution.py:210
  86.7 10.6 %collective-permute-start.28 = (bf16[128,384]{1,0:T(8,128)(2,1)S(1)}, bf16[128,384]{1,0:T(8,128)(2,1)S(1)}, u32[]{:S(2)}, u32[]{:S(2)}) collective-permute-start(bf16[128,384]{1,0:T(8,128)(2,1)S(1)} %get-tuple-element.57.rest_0_), channel_id=1, source_target_pairs={{0,4},{1,5},{2,6},{3,7},{4,0},{5,1},{6,2},{7,3},{8,12},{9,13},{10,... | collective-permute-start | bytes 294920 | tf_op jit(solution)/shard_map/ppermute | solution.py:210
  89.3 8.2 %collective-permute-start.29 = (bf16[128,384]{1,0:T(8,128)(2,1)S(1)}, bf16[128,384]{1,0:T(8,128)(2,1)S(1)}, u32[]{:S(2)}, u32[]{:S(2)}) collective-permute-start(bf16[128,384]{1,0:T(8,128)(2,1)S(1)} %get-tuple-element.57.rest_0_), channel_id=1, source_target_pairs={{0,6},{1,7},{2,4},{3,5},{4,2},{5,3},{6,0},{7,1},{8,14},{9,15},{10,... | collective-permute-start | bytes 294920 | tf_op jit(solution)/shard_map/ppermute | solution.py:210
  91.3 5.3 %collective-permute-start.24 = (f32[1,128]{1,0:T(1,128)S(1)}, f32[1,128]{1,0:T(1,128)S(1)}, u32[]{:S(2)}, u32[]{:S(2)}) collective-permute-start(f32[1,128]{1,0:T(1,128)S(1)} %add_add_fusion.2), channel_id=1, source_target_pairs={{0,4},{1,5},{2,6},{3,7},{4,0},{5,1},{6,2},{7,3},{8,12},{9,13},{10,... | collective-permute-start | bytes 1544 | tf_op jit(solution)/shard_map/ppermute | solution.py:210
  91.5 5.4 %collective-permute-start.25 = (f32[1,128]{1,0:T(1,128)S(1)}, f32[1,128]{1,0:T(1,128)S(1)}, u32[]{:S(2)}, u32[]{:S(2)}) collective-permute-start(f32[1,128]{1,0:T(1,128)S(1)} %add_add_fusion.2), channel_id=1, source_target_pairs={{0,6},{1,7},{2,4},{3,5},{4,2},{5,3},{6,0},{7,1},{8,14},{9,15},{10,... | collective-permute-start | bytes 1544 | tf_op jit(solution)/shard_map/ppermute | solution.py:210
  96.6 3.6 %collective-permute-start.23 = (f32[1,128]{1,0:T(1,128)S(1)}, f32[1,128]{1,0:T(1,128)S(1)}, u32[]{:S(2)}, u32[]{:S(2)}) collective-permute-start(f32[1,128]{1,0:T(1,128)S(1)} %add_add_fusion.2), channel_id=1, source_target_pairs={{0,2},{1,3},{2,0},{3,1},{4,6},{5,7},{6,4},{7,5},{8,10},{9,11},{10,... | collective-permute-start | bytes 1544 | tf_op jit(solution)/shard_map/ppermute | solution.py:210
  96.9 4.4 %collective-permute-start.30 = (bf16[128,384]{1,0:T(8,128)(2,1)S(1)}, bf16[128,384]{1,0:T(8,128)(2,1)S(1)}, u32[]{:S(2)}, u32[]{:S(2)}) collective-permute-start(bf16[128,384]{1,0:T(8,128)(2,1)S(1)} %get-tuple-element.57.rest_0_), channel_id=1, source_target_pairs={{0,1},{1,0},{2,3},{3,2},{4,5},{5,4},{6,7},{7,6},{8,9},{9,8},{10,11... | collective-permute-start | bytes 294920 | tf_op jit(solution)/shard_map/ppermute | solution.py:210
  96.9 4.5 %copy-start.10 = (bf16[128,384]{1,0:T(8,128)(2,1)}, bf16[128,384]{1,0:T(8,128)(2,1)S(1)}, u32[]{:S(2)}) copy-start(bf16[128,384]{1,0:T(8,128)(2,1)S(1)} %collective-permute-done.27.rest_1_) | copy-start | bytes 294916
  96.9 4.4 %collective-permute-start.31 = (bf16[128,384]{1,0:T(8,128)(2,1)S(1)}, bf16[128,384]{1,0:T(8,128)(2,1)S(1)}, u32[]{:S(2)}, u32[]{:S(2)}) collective-permute-start(bf16[128,384]{1,0:T(8,128)(2,1)S(1)} %collective-permute-done.27.rest_1_), channel_id=1, source_target_pairs={{0,1},{1,0},{2,3},{3,2},{4,5},{5,4},{6,7},{7,6},{8,9},{9,8},{10,11... | collective-permute-start | bytes 294920 | tf_op jit(solution)/shard_map/ppermute | solution.py:210
  97.4 4.0 %copy-start.11 = (bf16[128,384]{1,0:T(8,128)(2,1)}, bf16[128,384]{1,0:T(8,128)(2,1)S(1)}, u32[]{:S(2)}) copy-start(bf16[128,384]{1,0:T(8,128)(2,1)S(1)} %collective-permute-done.28.rest_2_) | copy-start | bytes 294916
  97.4 3.9 %collective-permute-start.32 = (bf16[128,384]{1,0:T(8,128)(2,1)S(1)}, bf16[128,384]{1,0:T(8,128)(2,1)S(1)}, u32[]{:S(2)}, u32[]{:S(2)}) collective-permute-start(bf16[128,384]{1,0:T(8,128)(2,1)S(1)} %collective-permute-done.28.rest_2_), channel_id=1, source_target_pairs={{0,1},{1,0},{2,3},{3,2},{4,5},{5,4},{6,7},{7,6},{8,9},{9,8},{10,11... | collective-permute-start | bytes 294920 | tf_op jit(solution)/shard_map/ppermute | solution.py:210
  97.5 3.9 %copy-start.12 = (bf16[128,384]{1,0:T(8,128)(2,1)}, bf16[128,384]{1,0:T(8,128)(2,1)S(1)}, u32[]{:S(2)}) copy-start(bf16[128,384]{1,0:T(8,128)(2,1)S(1)} %collective-permute-done.29.rest_3_) | copy-start | bytes 294916
  97.5 3.9 %collective-permute-start.33 = (bf16[128,384]{1,0:T(8,128)(2,1)S(1)}, bf16[128,384]{1,0:T(8,128)(2,1)S(1)}, u32[]{:S(2)}, u32[]{:S(2)}) collective-permute-start(bf16[128,384]{1,0:T(8,128)(2,1)S(1)} %collective-permute-done.29.rest_3_), channel_id=1, source_target_pairs={{0,1},{1,0},{2,3},{3,2},{4,5},{5,4},{6,7},{7,6},{8,9},{9,8},{10,11... | collective-permute-start | bytes 294920 | tf_op jit(solution)/shard_map/ppermute | solution.py:210
  100.1 1.3 %copy-start.17 = (f32[1,128]{1,0:T(1,128)}, f32[1,128]{1,0:T(1,128)S(1)}, u32[]{:S(2)}) copy-start(f32[1,128]{1,0:T(1,128)S(1)} %add_add_fusion.1.line) | copy-start | bytes 1540
  100.1 1.2 %collective-permute-start.26 = (f32[1,128]{1,0:T(1,128)S(1)}, f32[1,128]{1,0:T(1,128)S(1)}, u32[]{:S(2)}, u32[]{:S(2)}) collective-permute-start(f32[1,128]{1,0:T(1,128)S(1)} %add_add_fusion.1.line), channel_id=1, source_target_pairs={{0,1},{1,0},{2,3},{3,2},{4,5},{5,4},{6,7},{7,6},{8,9},{9,8},{10,11... | collective-permute-start | bytes 1544 | tf_op jit(solution)/shard_map/ppermute | solution.py:210
  (5 other events, 3.2 us)
